TPU v7x, 32 devices: a whole 2x2x4 slice. The times are simulated.
32 devices in a mesh: gx: 4 (over z), gy: 4 (over x, core), gz: 2 (over y).
Axes of the slice: x: 2, y: 2, z: 4, core: 2. Of those that a mesh axis runs over, the one named last changes fastest.
Arguments:
- krylov_basis: float32 [60, 16, 32, 256], P(None, 'gx', 'gy', 'gz'), may hold values from -6 to 6
- schur_vectors: float32 [60, 20], replicated, may hold values from -1 to 1, as said below
- next_vector: float32 [16, 32, 256], P('gx', 'gy', 'gz'), may hold values from -10 to 10
- diag_shift: float32 [16, 32, 256], P('gx', 'gy', 'gz'), may hold values from 0.25 to 2
- velocity: float32 [3, 16, 32, 256], P(None, 'gx', 'gy', 'gz'), may hold values from -1 to 1
Outputs:
- new_basis: float32 [24, 16, 32, 256], P(None, 'gx', 'gy', 'gz')
- hessenberg: float32 [24, 3], replicated
Inputs may be any that keep to these rules, and one draw needn't show every extreme that they name: `schur_vectors`: the columns are orthonormal.
All inputs are finite; a program needn't handle non-finite values.
Results may differ from a plain program's by a relative error of at most 0.0003.
Values sent between devices are 32-bit elements; how exact they have to be, the bound alone decides.
A program may use at most 64 MiB of HBM per device.

v0:
```python
import jax
import jax.numpy as jnp
from jax import lax
from jax.sharding import PartitionSpec as P

KEEP = 20
EXPAND = 3
ROWS = 24


def with_halo(value, sides, width):
    for axis, dim in sides:
        count, length = (lax.axis_size(axis), value.shape[dim])
        up = [(i, (i + 1) % count) for i in range(count - 1)]
        down = [(j, i) for i, j in up]
        last = lax.slice_in_dim(value, length - width, length, axis=dim)
        initial = lax.slice_in_dim(value, 0, width, axis=dim)
        before = lax.ppermute(last, axis, up)
        after = lax.ppermute(initial, axis, down)
        value = jnp.concatenate([before, value, after], axis=dim)
    return value


def combine_terms(
    field, x_ahead, x_behind, y_ahead, y_behind, z_ahead, z_behind, diag_shift, velocity
):
    neighbours = x_ahead + x_behind + y_ahead + y_behind + z_ahead + z_behind
    flow = (
        velocity[0] * (x_ahead - x_behind)
        + velocity[1] * (y_ahead - y_behind)
        + velocity[2] * (z_ahead - z_behind)
    )
    return (6.0 + diag_shift) * field - neighbours + 0.5 * flow


def operate_field(field, diag_shift, velocity):
    padded = with_halo(field, (("gx", 0), ("gy", 1), ("gz", 2)), 1)
    return combine_terms(
        field,
        padded[2:, 1:-1, 1:-1],
        padded[:-2, 1:-1, 1:-1],
        padded[1:-1, 2:, 1:-1],
        padded[1:-1, :-2, 1:-1],
        padded[1:-1, 1:-1, 2:],
        padded[1:-1, 1:-1, :-2],
        diag_shift,
        velocity,
    )


def per_device(krylov_basis, schur_vectors, next_vector, diag_shift, velocity):
    highest = lax.Precision.HIGHEST
    shape_local = next_vector.shape
    cell_count = (
        shape_local[0]
        * shape_local[1]
        * shape_local[2]
        * lax.axis_size("gx")
        * lax.axis_size("gy")
        * lax.axis_size("gz")
    )
    rotated = jnp.einsum("ik,ixyz->kxyz", schur_vectors, krylov_basis, precision=highest)
    columns = []
    starting = jnp.concatenate([rotated, next_vector[None]], axis=0)
    flat_start = starting.reshape(KEEP + 1, -1)
    gram_matrix = (
        lax.psum(jnp.dot(flat_start, flat_start.T, precision=highest), ("gx", "gy", "gz"))
        / cell_count
    )
    divisor = jnp.maximum(jnp.sqrt(gram_matrix[KEEP, KEEP]), 0.5)
    factor = jnp.ones((KEEP + 1,), jnp.float32).at[KEEP].set(1.0 / divisor)
    gram_matrix = gram_matrix * factor[:, None] * factor[None, :]
    vectors = jnp.concatenate([rotated, (next_vector / divisor)[None]], axis=0)
    for expansion in range(EXPAND):
        count = vectors.shape[0]
        flat_basis = vectors.reshape(count, -1)
        applied = operate_field(vectors[-1], diag_shift, velocity).reshape(-1)
        dotted, self_sum = lax.psum(
            (jnp.dot(flat_basis, applied, precision=highest), jnp.sum(applied * applied)),
            ("gx", "gy", "gz"),
        )
        first_coeffs = dotted / cell_count
        self_norm = self_sum / cell_count
        second_coeffs = first_coeffs - jnp.dot(gram_matrix, first_coeffs, precision=highest)
        total_coeffs = first_coeffs + second_coeffs
        partly = applied - jnp.dot(first_coeffs, flat_basis, precision=highest)
        cleaned = partly - jnp.dot(second_coeffs, flat_basis, precision=highest)
        length_sq = (
            self_norm
            - 2.0 * jnp.dot(total_coeffs, first_coeffs, precision=highest)
            + jnp.dot(
                total_coeffs,
                jnp.dot(gram_matrix, total_coeffs, precision=highest),
                precision=highest,
            )
        )
        length = jnp.sqrt(jnp.maximum(length_sq, 0.0))
        divisor = jnp.maximum(length, 0.5)
        column = jnp.zeros((ROWS,), jnp.float32)
        column = column.at[:count].set(total_coeffs).at[count].set(length)
        columns.append(column)
        newest = (cleaned / divisor).reshape(shape_local)
        vectors = jnp.concatenate([vectors, newest[None]], axis=0)
        intersect = (
            second_coeffs - jnp.dot(gram_matrix, second_coeffs, precision=highest)
        ) / divisor
        corner = jnp.maximum(length_sq, 0.0) / (divisor * divisor)
        upper_rows = jnp.concatenate([gram_matrix, intersect[:, None]], axis=1)
        lower_row = jnp.concatenate([intersect, corner[None]], axis=0)
        gram_matrix = jnp.concatenate([upper_rows, lower_row[None]], axis=0)
    return (vectors, jnp.stack(columns, axis=1))


def solution(mesh):
    in_specs = (
        P(None, "gx", "gy", "gz"),
        P(),
        P("gx", "gy", "gz"),
        P("gx", "gy", "gz"),
        P(None, "gx", "gy", "gz"),
    )
    out_specs = (P(None, "gx", "gy", "gz"), P())
    return jax.shard_map(
        per_device, mesh=mesh, in_specs=in_specs, out_specs=out_specs, check_vma=False
    )
```

profile of v0, /device:TPU:0, one launch (start us, length us, event | category | flops | bytes accessed | tf_op | source)
XLA Modules:
  0.0 258.3 jit_solution(9260418553971904028)
XLA Ops:
  0.7 1.2 copy-done
  1.8 1.9 fusion.10
  4.2 42.1 %psum.49 = f32[21,21]{1,0:T(8,128)S(1)} all-reduce(f32[21,21]{1,0:T(8,128)S(1)} %convolution_bitcast_fusion), channel_id=1, replica_groups=mesh['gx'=4,'gy'=4,'gz'=2] {'gx','gy','gz'}, use_global_device_ids=true, to_apply=%region_0.0 | all-reduce | flops 441 | bytes 3528 | tf_op jit(solution)/shard_map/psum | solution.py:67
  47.6 1.3 collective-permute-start
  48.9 4.5 %collective-permute-start.1 = (f32[1,8,128]{2,1,0:T(8,128)S(1)}, f32[1,8,128]{2,1,0:T(8,128)S(1)}, u32[]{:S(2)}, u32[]{:S(2)}) collective-permute-start(f32[1,8,128]{2,1,0:T(8,128)S(1)} %get-tuple-element.124), channel_id=1, source_target_pairs={{0,8},{8,16},{16,24},{1,9},{9,17},{17,25},{2,10},{10,18},{18,26},{... | collective-permute-start | bytes 12296 | tf_op jit(solution)/shard_map/ppermute | solution.py:18
  53.7 1.1 collective-permute-done.1
  54.8 1.3 collective-permute-start.2
  56.1 3.0 %collective-permute-start.3 = (f32[6,1,128]{2,1,0:T(1,128)S(1)}, f32[6,1,128]{2,1,0:T(1,128)S(1)}, u32[]{:S(2)}, u32[]{:S(2)}) collective-permute-start(f32[6,1,128]{2,1,0:T(1,128)S(1)} %get-tuple-element.118), channel_id=1, source_target_pairs={{0,2},{2,4},{4,6},{1,3},{3,5},{5,7},{8,10},{10,12},{12,14},{9,11},... | collective-permute-start | bytes 9224 | tf_op jit(solution)/shard_map/ppermute | solution.py:18
  60.0 4.2 %collective-permute-start.5 = (f32[6,10,1]{2,1,0:T(8,128)S(1)}, f32[6,10,1]{2,1,0:T(8,128)S(1)}, u32[]{:S(2)}, u32[]{:S(2)}) collective-permute-start(f32[6,10,1]{2,1,0:T(8,128)S(1)} %get-tuple-element.113), channel_id=1, source_target_pairs={{0,1},{2,3},{4,5},{6,7},{8,9},{10,11},{12,13},{14,15},{16,17},{18,... | collective-permute-start | bytes 728 | tf_op jit(solution)/shard_map/ppermute | solution.py:18
  64.2 1.3 collective-permute-start.4
  66.0 4.3 %collective-permute-done.4 = f32[6,10,1]{2,1,0:T(8,128)S(1)} collective-permute-done((f32[6,10,1]{2,1,0:T(8,128)S(1)}, f32[6,10,1]{2,1,0:T(8,128)S(1)}, u32[]{:S(2)}, u32[]{:S(2)}) %collective-permute-start.4) | collective-permute-done | bytes 272 | tf_op jit(solution)/shard_map/ppermute | solution.py:19
  71.4 40.6 %all-reduce.6 = (f32[21]{0:T(128)S(1)}, f32[]{:T(128)}) all-reduce(f32[21]{0:T(128)S(1)} %convolution_bitcast_fusion.11, f32[]{:T(128)} %get-tuple-element.106), channel_id=1, replica_groups=mesh['gx'=4,'gy'=4,'gz'=2] {'gx','gy','gz'}, use_global_device_ids=true, to_apply=%region_1.0 | all-reduce | flops 22 | bytes 176 | tf_op jit(solution)/shard_map/psum | solution.py:78
  116.3 1.3 collective-permute-start.6
  117.6 4.5 %collective-permute-start.7 = (f32[1,8,128]{2,1,0:T(8,128)S(1)}, f32[1,8,128]{2,1,0:T(8,128)S(1)}, u32[]{:S(2)}, u32[]{:S(2)}) collective-permute-start(f32[1,8,128]{2,1,0:T(8,128)S(1)} %get-tuple-element.122), channel_id=1, source_target_pairs={{0,8},{8,16},{16,24},{1,9},{9,17},{17,25},{2,10},{10,18},{18,26},{... | collective-permute-start | bytes 12296 | tf_op jit(solution)/shard_map/ppermute | solution.py:18
  122.5 1.0 collective-permute-done.7
  123.5 1.3 collective-permute-start.8
  124.8 3.0 %collective-permute-start.9 = (f32[6,1,128]{2,1,0:T(1,128)S(1)}, f32[6,1,128]{2,1,0:T(1,128)S(1)}, u32[]{:S(2)}, u32[]{:S(2)}) collective-permute-start(f32[6,1,128]{2,1,0:T(1,128)S(1)} %get-tuple-element.116), channel_id=1, source_target_pairs={{0,2},{2,4},{4,6},{1,3},{3,5},{5,7},{8,10},{10,12},{12,14},{9,11},... | collective-permute-start | bytes 9224 | tf_op jit(solution)/shard_map/ppermute | solution.py:18
  127.8 0.8 collective-permute-done.9
  128.7 4.4 %collective-permute-start.11 = (f32[6,10,1]{2,1,0:T(8,128)S(1)}, f32[6,10,1]{2,1,0:T(8,128)S(1)}, u32[]{:S(2)}, u32[]{:S(2)}) collective-permute-start(f32[6,10,1]{2,1,0:T(8,128)S(1)} %get-tuple-element.111), channel_id=1, source_target_pairs={{0,1},{2,3},{4,5},{6,7},{8,9},{10,11},{12,13},{14,15},{16,17},{18,... | collective-permute-start | bytes 728 | tf_op jit(solution)/shard_map/ppermute | solution.py:18
  133.1 1.3 collective-permute-start.10
  134.8 4.5 %collective-permute-done.10 = f32[6,10,1]{2,1,0:T(8,128)S(1)} collective-permute-done((f32[6,10,1]{2,1,0:T(8,128)S(1)}, f32[6,10,1]{2,1,0:T(8,128)S(1)}, u32[]{:S(2)}, u32[]{:S(2)}) %collective-permute-start.10) | collective-permute-done | bytes 272 | tf_op jit(solution)/shard_map/ppermute | solution.py:19
  140.5 41.6 %all-reduce.5 = (f32[22]{0:T(128)S(1)}, f32[]{:T(128)}) all-reduce(f32[22]{0:T(128)S(1)} %convolution_bitcast_fusion.10, f32[]{:T(128)} %get-tuple-element.102), channel_id=1, replica_groups=mesh['gx'=4,'gy'=4,'gz'=2] {'gx','gy','gz'}, use_global_device_ids=true, to_apply=%region_4.0 | all-reduce | flops 23 | bytes 184 | tf_op jit(solution)/shard_map/psum | solution.py:78
  186.5 1.3 collective-permute-start.12
  187.8 4.5 %collective-permute-start.13 = (f32[1,8,128]{2,1,0:T(8,128)S(1)}, f32[1,8,128]{2,1,0:T(8,128)S(1)}, u32[]{:S(2)}, u32[]{:S(2)}) collective-permute-start(f32[1,8,128]{2,1,0:T(8,128)S(1)} %get-tuple-element.120), channel_id=1, source_target_pairs={{0,8},{8,16},{16,24},{1,9},{9,17},{17,25},{2,10},{10,18},{18,26},{... | collective-permute-start | bytes 12296 | tf_op jit(solution)/shard_map/ppermute | solution.py:18
  192.6 1.0 collective-permute-done.13
  193.7 1.3 collective-permute-start.14
  195.0 3.0 %collective-permute-start.15 = (f32[6,1,128]{2,1,0:T(1,128)S(1)}, f32[6,1,128]{2,1,0:T(1,128)S(1)}, u32[]{:S(2)}, u32[]{:S(2)}) collective-permute-start(f32[6,1,128]{2,1,0:T(1,128)S(1)} %get-tuple-element.114), channel_id=1, source_target_pairs={{0,2},{2,4},{4,6},{1,3},{3,5},{5,7},{8,10},{10,12},{12,14},{9,11},... | collective-permute-start | bytes 9224 | tf_op jit(solution)/shard_map/ppermute | solution.py:18
  198.9 4.4 %collective-permute-start.17 = (f32[6,10,1]{2,1,0:T(8,128)S(1)}, f32[6,10,1]{2,1,0:T(8,128)S(1)}, u32[]{:S(2)}, u32[]{:S(2)}) collective-permute-start(f32[6,10,1]{2,1,0:T(8,128)S(1)} %get-tuple-element.109), channel_id=1, source_target_pairs={{0,1},{2,3},{4,5},{6,7},{8,9},{10,11},{12,13},{14,15},{16,17},{18,... | collective-permute-start | bytes 728 | tf_op jit(solution)/shard_map/ppermute | solution.py:18
  203.3 1.3 collective-permute-start.16
  205.0 4.5 %collective-permute-done.16 = f32[6,10,1]{2,1,0:T(8,128)S(1)} collective-permute-done((f32[6,10,1]{2,1,0:T(8,128)S(1)}, f32[6,10,1]{2,1,0:T(8,128)S(1)}, u32[]{:S(2)}, u32[]{:S(2)}) %collective-permute-start.16) | collective-permute-done | bytes 272 | tf_op jit(solution)/shard_map/ppermute | solution.py:19
  210.7 41.6 %all-reduce.4 = (f32[23]{0:T(128)S(1)}, f32[]{:T(128)}) all-reduce(f32[23]{0:T(128)S(1)} %convolution_bitcast_fusion.9, f32[]{:T(128)} %get-tuple-element.98), channel_id=1, replica_groups=mesh['gx'=4,'gy'=4,'gz'=2] {'gx','gy','gz'}, use_global_device_ids=true, to_apply=%region_7.0 | all-reduce | flops 24 | bytes 192 | tf_op jit(solution)/shard_map/psum | solution.py:78
  256.8 0.8 copy.15
  (76 shorter events, 16.3 us)
Async XLA Ops:
  0.6 1.2 copy-start
  0.6 3.1 %copy-start.3 = (f32[4,8,128]{2,1,0:T(8,128)S(1)}, f32[4,8,128]{2,1,0:T(8,128)}, u32[]{:S(2)}) copy-start(f32[4,8,128]{2,1,0:T(8,128)} %param.21) | copy-start | bytes 49156
  47.6 6.1 %collective-permute-start = (f32[1,8,128]{2,1,0:T(8,128)S(1)}, f32[1,8,128]{2,1,0:T(8,128)S(1)}, u32[]{:S(2)}, u32[]{:S(2)}) collective-permute-start(f32[1,8,128]{2,1,0:T(8,128)S(1)} %get-tuple-element.125), channel_id=1, source_target_pairs={{8,0},{16,8},{24,16},{9,1},{17,9},{25,17},{10,2},{18,10},{26,18},{... | collective-permute-start | bytes 12296 | tf_op jit(solution)/shard_map/ppermute | solution.py:19
  48.9 5.9 %collective-permute-start.1 = (f32[1,8,128]{2,1,0:T(8,128)S(1)}, f32[1,8,128]{2,1,0:T(8,128)S(1)}, u32[]{:S(2)}, u32[]{:S(2)}) collective-permute-start(f32[1,8,128]{2,1,0:T(8,128)S(1)} %get-tuple-element.124), channel_id=1, source_target_pairs={{0,8},{8,16},{16,24},{1,9},{9,17},{17,25},{2,10},{10,18},{18,26},{... | collective-permute-start | bytes 12296 | tf_op jit(solution)/shard_map/ppermute | solution.py:18
  54.8 4.5 %collective-permute-start.2 = (f32[6,1,128]{2,1,0:T(1,128)S(1)}, f32[6,1,128]{2,1,0:T(1,128)S(1)}, u32[]{:S(2)}, u32[]{:S(2)}) collective-permute-start(f32[6,1,128]{2,1,0:T(1,128)S(1)} %get-tuple-element.119), channel_id=1, source_target_pairs={{2,0},{4,2},{6,4},{3,1},{5,3},{7,5},{10,8},{12,10},{14,12},{11,9},... | collective-permute-start | bytes 9224 | tf_op jit(solution)/shard_map/ppermute | solution.py:19
  56.1 3.8 %collective-permute-start.3 = (f32[6,1,128]{2,1,0:T(1,128)S(1)}, f32[6,1,128]{2,1,0:T(1,128)S(1)}, u32[]{:S(2)}, u32[]{:S(2)}) collective-permute-start(f32[6,1,128]{2,1,0:T(1,128)S(1)} %get-tuple-element.118), channel_id=1, source_target_pairs={{0,2},{2,4},{4,6},{1,3},{3,5},{5,7},{8,10},{10,12},{12,14},{9,11},... | collective-permute-start | bytes 9224 | tf_op jit(solution)/shard_map/ppermute | solution.py:18
  60.0 5.9 %collective-permute-start.5 = (f32[6,10,1]{2,1,0:T(8,128)S(1)}, f32[6,10,1]{2,1,0:T(8,128)S(1)}, u32[]{:S(2)}, u32[]{:S(2)}) collective-permute-start(f32[6,10,1]{2,1,0:T(8,128)S(1)} %get-tuple-element.113), channel_id=1, source_target_pairs={{0,1},{2,3},{4,5},{6,7},{8,9},{10,11},{12,13},{14,15},{16,17},{18,... | collective-permute-start | bytes 728 | tf_op jit(solution)/shard_map/ppermute | solution.py:18
  64.2 6.0 %collective-permute-start.4 = (f32[6,10,1]{2,1,0:T(8,128)S(1)}, f32[6,10,1]{2,1,0:T(8,128)S(1)}, u32[]{:S(2)}, u32[]{:S(2)}) collective-permute-start(f32[6,10,1]{2,1,0:T(8,128)S(1)} %get-tuple-element.112), channel_id=1, source_target_pairs={{1,0},{3,2},{5,4},{7,6},{9,8},{11,10},{13,12},{15,14},{17,16},{19,... | collective-permute-start | bytes 728 | tf_op jit(solution)/shard_map/ppermute | solution.py:19
  65.6 4.6 %copy-start.1 = (f32[3,4,8,128]{3,2,1,0:T(8,128)S(1)}, f32[3,4,8,128]{3,2,1,0:T(8,128)}, u32[]{:S(2)}) copy-start(f32[3,4,8,128]{3,2,1,0:T(8,128)} %param.23) | copy-start | bytes 147460
  65.6 4.6 %copy-start.2 = (f32[4,8,128]{2,1,0:T(8,128)S(1)}, f32[4,8,128]{2,1,0:T(8,128)}, u32[]{:S(2)}) copy-start(f32[4,8,128]{2,1,0:T(8,128)} %param.22) | copy-start | bytes 49156
  116.3 6.2 %collective-permute-start.6 = (f32[1,8,128]{2,1,0:T(8,128)S(1)}, f32[1,8,128]{2,1,0:T(8,128)S(1)}, u32[]{:S(2)}, u32[]{:S(2)}) collective-permute-start(f32[1,8,128]{2,1,0:T(8,128)S(1)} %get-tuple-element.123), channel_id=1, source_target_pairs={{8,0},{16,8},{24,16},{9,1},{17,9},{25,17},{10,2},{18,10},{26,18},{... | collective-permute-start | bytes 12296 | tf_op jit(solution)/shard_map/ppermute | solution.py:19
  117.6 5.9 %collective-permute-start.7 = (f32[1,8,128]{2,1,0:T(8,128)S(1)}, f32[1,8,128]{2,1,0:T(8,128)S(1)}, u32[]{:S(2)}, u32[]{:S(2)}) collective-permute-start(f32[1,8,128]{2,1,0:T(8,128)S(1)} %get-tuple-element.122), channel_id=1, source_target_pairs={{0,8},{8,16},{16,24},{1,9},{9,17},{17,25},{2,10},{10,18},{18,26},{... | collective-permute-start | bytes 12296 | tf_op jit(solution)/shard_map/ppermute | solution.py:18
  123.5 4.3 %collective-permute-start.8 = (f32[6,1,128]{2,1,0:T(1,128)S(1)}, f32[6,1,128]{2,1,0:T(1,128)S(1)}, u32[]{:S(2)}, u32[]{:S(2)}) collective-permute-start(f32[6,1,128]{2,1,0:T(1,128)S(1)} %get-tuple-element.117), channel_id=1, source_target_pairs={{2,0},{4,2},{6,4},{3,1},{5,3},{7,5},{10,8},{12,10},{14,12},{11,9},... | collective-permute-start | bytes 9224 | tf_op jit(solution)/shard_map/ppermute | solution.py:19
  124.8 3.8 %collective-permute-start.9 = (f32[6,1,128]{2,1,0:T(1,128)S(1)}, f32[6,1,128]{2,1,0:T(1,128)S(1)}, u32[]{:S(2)}, u32[]{:S(2)}) collective-permute-start(f32[6,1,128]{2,1,0:T(1,128)S(1)} %get-tuple-element.116), channel_id=1, source_target_pairs={{0,2},{2,4},{4,6},{1,3},{3,5},{5,7},{8,10},{10,12},{12,14},{9,11},... | collective-permute-start | bytes 9224 | tf_op jit(solution)/shard_map/ppermute | solution.py:18
  128.7 6.1 %collective-permute-start.11 = (f32[6,10,1]{2,1,0:T(8,128)S(1)}, f32[6,10,1]{2,1,0:T(8,128)S(1)}, u32[]{:S(2)}, u32[]{:S(2)}) collective-permute-start(f32[6,10,1]{2,1,0:T(8,128)S(1)} %get-tuple-element.111), channel_id=1, source_target_pairs={{0,1},{2,3},{4,5},{6,7},{8,9},{10,11},{12,13},{14,15},{16,17},{18,... | collective-permute-start | bytes 728 | tf_op jit(solution)/shard_map/ppermute | solution.py:18
  133.1 6.3 %collective-permute-start.10 = (f32[6,10,1]{2,1,0:T(8,128)S(1)}, f32[6,10,1]{2,1,0:T(8,128)S(1)}, u32[]{:S(2)}, u32[]{:S(2)}) collective-permute-start(f32[6,10,1]{2,1,0:T(8,128)S(1)} %get-tuple-element.110), channel_id=1, source_target_pairs={{1,0},{3,2},{5,4},{7,6},{9,8},{11,10},{13,12},{15,14},{17,16},{19,... | collective-permute-start | bytes 728 | tf_op jit(solution)/shard_map/ppermute | solution.py:19
  186.5 6.2 %collective-permute-start.12 = (f32[1,8,128]{2,1,0:T(8,128)S(1)}, f32[1,8,128]{2,1,0:T(8,128)S(1)}, u32[]{:S(2)}, u32[]{:S(2)}) collective-permute-start(f32[1,8,128]{2,1,0:T(8,128)S(1)} %get-tuple-element.121), channel_id=1, source_target_pairs={{8,0},{16,8},{24,16},{9,1},{17,9},{25,17},{10,2},{18,10},{26,18},{... | collective-permute-start | bytes 12296 | tf_op jit(solution)/shard_map/ppermute | solution.py:19
  187.8 5.9 %collective-permute-start.13 = (f32[1,8,128]{2,1,0:T(8,128)S(1)}, f32[1,8,128]{2,1,0:T(8,128)S(1)}, u32[]{:S(2)}, u32[]{:S(2)}) collective-permute-start(f32[1,8,128]{2,1,0:T(8,128)S(1)} %get-tuple-element.120), channel_id=1, source_target_pairs={{0,8},{8,16},{16,24},{1,9},{9,17},{17,25},{2,10},{10,18},{18,26},{... | collective-permute-start | bytes 12296 | tf_op jit(solution)/shard_map/ppermute | solution.py:18
  193.7 4.3 %collective-permute-start.14 = (f32[6,1,128]{2,1,0:T(1,128)S(1)}, f32[6,1,128]{2,1,0:T(1,128)S(1)}, u32[]{:S(2)}, u32[]{:S(2)}) collective-permute-start(f32[6,1,128]{2,1,0:T(1,128)S(1)} %get-tuple-element.115), channel_id=1, source_target_pairs={{2,0},{4,2},{6,4},{3,1},{5,3},{7,5},{10,8},{12,10},{14,12},{11,9},... | collective-permute-start | bytes 9224 | tf_op jit(solution)/shard_map/ppermute | solution.py:19
  195.0 3.8 %collective-permute-start.15 = (f32[6,1,128]{2,1,0:T(1,128)S(1)}, f32[6,1,128]{2,1,0:T(1,128)S(1)}, u32[]{:S(2)}, u32[]{:S(2)}) collective-permute-start(f32[6,1,128]{2,1,0:T(1,128)S(1)} %get-tuple-element.114), channel_id=1, source_target_pairs={{0,2},{2,4},{4,6},{1,3},{3,5},{5,7},{8,10},{10,12},{12,14},{9,11},... | collective-permute-start | bytes 9224 | tf_op jit(solution)/shard_map/ppermute | solution.py:18
  198.9 6.1 %collective-permute-start.17 = (f32[6,10,1]{2,1,0:T(8,128)S(1)}, f32[6,10,1]{2,1,0:T(8,128)S(1)}, u32[]{:S(2)}, u32[]{:S(2)}) collective-permute-start(f32[6,10,1]{2,1,0:T(8,128)S(1)} %get-tuple-element.109), channel_id=1, source_target_pairs={{0,1},{2,3},{4,5},{6,7},{8,9},{10,11},{12,13},{14,15},{16,17},{18,... | collective-permute-start | bytes 728 | tf_op jit(solution)/shard_map/ppermute | solution.py:18
  203.3 6.3 %collective-permute-start.16 = (f32[6,10,1]{2,1,0:T(8,128)S(1)}, f32[6,10,1]{2,1,0:T(8,128)S(1)}, u32[]{:S(2)}, u32[]{:S(2)}) collective-permute-start(f32[6,10,1]{2,1,0:T(8,128)S(1)} %get-tuple-element.108), channel_id=1, source_target_pairs={{1,0},{3,2},{5,4},{7,6},{9,8},{11,10},{13,12},{15,14},{17,16},{19,... | collective-permute-start | bytes 728 | tf_op jit(solution)/shard_map/ppermute | solution.py:19
where the time goes:
time: 260 us; the launch traced here: 258 us
  blocking collectives  166 us (64%)
  starting transfers between devices  47.2 us (18%)
  waiting for transfers between devices  19.5 us (8%)
  matrix products  10.7 us (4%)
  between operations  7.79 us (3%)
  local copies, waits for them, and re-layouts  4 us (2%)
  other arithmetic  3.24 us (1%)
    psum x3, blocking collectives, per_device(): lax.psum((jnp.dot(flat_basis, applied, precision=highest), jnp.sum(applie...  124 us
    psum x1, blocking collectives, per_device(): lax.psum(jnp.dot(flat_start, flat_start.T, precision=highest), ('gx', 'gy...  42.1 us
    ppermute x9, starting transfers between devices, with_halo(): before = lax.ppermute(last, axis, up)  35.6 us
    ppermute x9, waiting for transfers between devices, with_halo(): after = lax.ppermute(initial, axis, down)  13.4 us
    ppermute x9, starting transfers between devices, with_halo(): after = lax.ppermute(initial, axis, down)  11.6 us
    ppermute x9, waiting for transfers between devices, with_halo(): before = lax.ppermute(last, axis, up)  6.12 us
  transfers between devices with their start and end apart: 18, of which 12 were waited for; matrix products, arithmetic and copies ran while one was open for 0% of the time, Pallas kernels for 0%

commit v1 on v0

v1 whole, which is shorter than its diff:
```python
import functools

import jax
import jax.numpy as jnp
from jax import lax
from jax.experimental import pallas as pl
from jax.experimental.pallas import tpu as pltpu
from jax.sharding import PartitionSpec as P

KEEP = 20
EXPAND = 3
ROWS = 24
LANES = 128
GROUP = 32
AXES = ("gx", "gy", "gz")


def group_partner(phase, offset, place, sizes):
    ix, iy, iz = place
    nx, ny, nz = sizes
    if phase == 1:
        return (lax.rem(ix + offset, nx), iy, iz)
    other = lax.rem(iy * nz + iz + offset, ny * nz)
    return (ix, other // nz, lax.rem(other, nz))


def body(
    sizes, cells,
    kry_hbm, schur, w_ref, diag, vel,
    out, hess,
    kry, image, xr, yr, zr, ypack, zpack, xh, yh, zh, xs, ys, zs,
    gsend, grecv0, grecv1, rsend, rrecv0, rrecv1,
    load_sem, halo_send, halo_recv, gsem_s0, gsem_r0, gsem_s1, gsem_r1,
    rsem_s0, rsem_r0, rsem_s1, rsem_r1,
):
    place = tuple(lax.axis_index(a) for a in AXES)
    basis = kry.shape[0]
    bx, by, bz = w_ref.shape
    load = pltpu.make_async_copy(kry_hbm, kry, load_sem)
    load.start()
    groups = (sizes[1] * sizes[2], sizes[0])

    for ref in (xr, yr, zr, xs, ys, zs):
        ref[...] = jnp.zeros_like(ref)
    out[KEEP + 1:ROWS] = jnp.zeros((ROWS - KEEP - 1, bx, by, bz), jnp.float32)
    out[KEEP] = w_ref[...]

    barrier = pltpu.get_barrier_semaphore()
    for phase in (0, 1):
        for offset in range(1, groups[phase]):
            pl.semaphore_signal(
                barrier, inc=1,
                device_id=group_partner(phase, offset, place, sizes),
                device_id_type=pl.DeviceIdType.MESH,
            )
    pl.semaphore_wait(barrier, groups[0] + groups[1] - 2)

    def halo_copies(kind, sources, targets):
        found = []
        for d in range(3):
            for side in (0, 1):
                at = (kind * 3 + d) * 2 + side
                to = list(place)
                to[d] = place[d] + (1 if side == 0 else -1)
                can_send = place[d] < sizes[d] - 1 if side == 0 else place[d] > 0
                can_recv = place[d] > 0 if side == 0 else place[d] < sizes[d] - 1
                found.append((
                    pltpu.make_async_remote_copy(
                        src_ref=sources[d][side], dst_ref=targets[d][side],
                        send_sem=halo_send.at[at], recv_sem=halo_recv.at[at],
                        device_id=tuple(to), device_id_type=pl.DeviceIdType.MESH,
                    ), can_send, can_recv))
        return found

    def halo_start(copies):
        for copy, can_send, _ in copies:
            pl.when(can_send)(copy.start)

    def halo_wait(copies):
        for copy, _, can_recv in copies:
            pl.when(can_recv)(copy.wait_recv)

    def halo_finish(copies):
        for copy, can_send, _ in copies:
            pl.when(can_send)(copy.wait_send)

    def field_copies(kind, ref):
        return halo_copies(
            kind,
            ((ref.at[bx - 1], ref.at[0]), (ref, ref), (ref, ref)),
            tuple((r.at[kind, 0], r.at[kind, 1]) for r in (xs, ys, zs)),
        )

    def exchange(send, slots, sems_s, sems_r, phase):
        copies = []
        for offset in range(1, groups[phase]):
            copies.append(pltpu.make_async_remote_copy(
                src_ref=send, dst_ref=slots.at[offset - 1],
                send_sem=sems_s.at[offset - 1], recv_sem=sems_r.at[offset - 1],
                device_id=group_partner(phase, offset, place, sizes),
                device_id_type=pl.DeviceIdType.MESH,
            ))
        for copy in copies:
            copy.start()
        return copies

    def gather_sum(copies, own, slots):
        for copy in copies:
            copy.wait_recv()
        for k in range(len(copies)):
            own = own + slots[k]
        return own

    lane3 = lax.broadcasted_iota(jnp.int32, (by, bz), 1)
    row3 = lax.broadcasted_iota(jnp.int32, (by, bz), 0)

    def stencil(v, x_before, x_after, y_before, y_after, z_before, z_after):
        res = []
        for x in range(bx):
            here = v[x]
            xb = v[x - 1] if x > 0 else x_before
            xa = v[x + 1] if x < bx - 1 else x_after
            yb = jnp.where(row3 == 0, y_before[x], pltpu.roll(here, 1, 0))
            ya = jnp.where(row3 == by - 1, y_after[x], pltpu.roll(here, by - 1, 0))
            zb = jnp.where(lane3 == 0, z_before[x], pltpu.roll(here, 1, 1))
            za = jnp.where(lane3 == bz - 1, z_after[x], pltpu.roll(here, bz - 1, 1))
            neighbours = xa + xb + ya + yb + za + zb
            flow = (vel[0, x] * (xa - xb) + vel[1, x] * (ya - yb) + vel[2, x] * (za - zb))
            res.append((6.0 + diag[x]) * here - neighbours + 0.5 * flow)
        return res

    def dots(v, count):
        parts = []
        for i in range(ROWS):
            if i < count:
                total = out[i, 0] * v[0]
                for x in range(1, bx):
                    total = total + out[i, x] * v[x]
            elif i == ROWS - 1:
                total = v[0] * v[0]
                for x in range(1, bx):
                    total = total + v[x] * v[x]
            else:
                total = None
            parts.append(jnp.zeros((1, bz), jnp.float32) if total is None
                         else jnp.sum(total, axis=0, keepdims=True))
        return jnp.sum(jnp.concatenate(parts, axis=0), axis=1, keepdims=True)

    halo_w = field_copies(0, w_ref)
    halo_start(halo_w)

    load.wait()
    wide, deep = 5, 4
    for first in range(0, KEEP, wide):
        def step(at, sums, first=first):
            sums = list(sums)
            for k in range(deep):
                i = at * deep + k
                for x in range(bx):
                    tile = kry[i, x]
                    for j in range(wide):
                        sums[j * bx + x] = sums[j * bx + x] + schur[i, first + j] * tile
            return tuple(sums)
        sums = lax.fori_loop(
            0, basis // deep, step,
            tuple(jnp.zeros((by, bz), jnp.float32) for _ in range(wide * bx)))
        for j in range(wide):
            for x in range(bx):
                out[first + j, x] = sums[j * bx + x]

    for side, (row, edge) in enumerate(((by - 1, bz - 1), (0, 0))):
        for i in range(KEEP):
            ypack[side, i] = out[i, :, row, :]
        for x in range(bx):
            packed = jnp.zeros((by, bz), jnp.float32)
            for i in range(KEEP):
                packed = jnp.where(
                    lane3 == i, pltpu.roll(out[i, x], (i - edge) % bz, 1), packed)
            zpack[side, x] = packed
    halo_r = halo_copies(
        3,
        ((out.at[0:KEEP, bx - 1], out.at[0:KEEP, 0]), (ypack.at[0], ypack.at[1]),
         (zpack.at[0], zpack.at[1])),
        tuple((r.at[0], r.at[1]) for r in (xr, yr, zr)),
    )
    halo_start(halo_r)

    row = lax.broadcasted_iota(jnp.int32, (ROWS, LANES), 0)
    lane = lax.broadcasted_iota(jnp.int32, (ROWS, LANES), 1)
    lane1 = lax.broadcasted_iota(jnp.int32, (1, LANES), 1)
    row1 = lax.broadcasted_iota(jnp.int32, (ROWS, 1), 0)

    gram = jnp.zeros((ROWS, LANES), jnp.float32)
    for j in range(KEEP + 1):
        col = dots([out[j, x] for x in range(bx)], KEEP + 1)
        gram = jnp.where(lane == j, jnp.where(row < KEEP + 1, col, 0.0), gram)

    halo_wait(halo_w)
    applied = stencil(
        [w_ref[x] for x in range(bx)], xs[0, 0], xs[0, 1],
        [ys[0, 0, x, by - 1:by, :] for x in range(bx)],
        [ys[0, 1, x, 0:1, :] for x in range(bx)],
        [zs[0, 0, x, :, bz - 1:bz] for x in range(bx)],
        [zs[0, 1, x, :, 0:1] for x in range(bx)],
    )
    for x in range(bx):
        image[0, x] = applied[x]
    halo_a = field_copies(1, image.at[0])
    halo_start(halo_a)
    col = dots(applied, KEEP + 1)
    gram = jnp.where(lane == ROWS - 1, col, gram)
    packed = jnp.zeros((8, LANES), jnp.float32)
    for part in range(ROWS // 8):
        piece = gram[part * 8:part * 8 + 8]
        packed = packed + (pltpu.roll(piece, part * GROUP, 1) if part else piece)
    gsend[0] = packed
    copies0 = exchange(gsend.at[0], grecv0, gsem_s0, gsem_r0, 0)
    packed = gather_sum(copies0, packed, grecv0)
    gsend[1] = packed
    copies1 = exchange(gsend.at[1], grecv1, gsem_s1, gsem_r1, 1)
    packed = gather_sum(copies1, packed, grecv1) * (1.0 / cells)
    pending = [copies0, copies1]
    gram = jnp.concatenate(
        [packed] + [pltpu.roll(packed, LANES - part * GROUP, 1) for part in range(1, ROWS // 8)],
        axis=0)

    c_col = jnp.sum(jnp.where(lane == ROWS - 1, gram, 0.0), axis=1, keepdims=True)
    gram = jnp.where((lane < KEEP + 1) & (row < KEEP + 1), gram, 0.0)
    norm_sq = jnp.sum(
        jnp.sum(jnp.where((lane == KEEP) & (row == KEEP), gram, 0.0), axis=1, keepdims=True),
        axis=0, keepdims=True)
    scale = 1.0 / jnp.maximum(jnp.sqrt(norm_sq), 0.5)
    gram = gram * jnp.where(row == KEEP, scale, 1.0) * jnp.where(lane == KEEP, scale, 1.0)
    c_col = c_col * scale * jnp.where((row1 == KEEP) | (row1 == ROWS - 1), scale, 1.0)
    for x in range(bx):
        out[KEEP, x] = w_ref[x] * scale
    applied = [tile * scale for tile in applied]

    halo_wait(halo_r)
    for side in (0, 1):
        near_row, near_lane = (by - 1, bz - 1) if side == 0 else (0, 0)
        xh[side, 0] = xs[0, side] * scale
        for x in range(bx):
            yh[side, 0, x:x + 1] = ys[0, side, x, near_row:near_row + 1, :] * scale
            zh[side, x] = jnp.where(
                lane3 == KEEP, zs[0, side, x, :, near_lane:near_lane + 1] * scale, zr[side, x])
    halos = {1: halo_a}
    hcols = []
    for k in range(EXPAND):
        count = KEEP + 1 + k
        if k > 0:
            rowform = jnp.sum(jnp.where(row == lane, dots(applied, count), 0.0),
                              axis=0, keepdims=True)
            rsend[k - 1, 0] = rowform
            copies0 = exchange(rsend.at[k - 1, 0], rrecv0.at[k - 1],
                               rsem_s0.at[k - 1], rsem_r0.at[k - 1], 0)
            rowform = gather_sum(copies0, rowform, rrecv0.at[k - 1])
            rsend[k - 1, 1] = rowform
            copies1 = exchange(rsend.at[k - 1, 1], rrecv1.at[k - 1],
                               rsem_s1.at[k - 1], rsem_r1.at[k - 1], 1)
            rowform = gather_sum(copies1, rowform, rrecv1.at[k - 1]) * (1.0 / cells)
            pending += [copies0, copies1]
            c_col = jnp.sum(jnp.where(row == lane, rowform, 0.0), axis=1, keepdims=True)
        else:
            rowform = jnp.sum(jnp.where(row == lane, c_col, 0.0), axis=0, keepdims=True)
        self_norm = jnp.sum(jnp.where(lane1 == ROWS - 1, rowform, 0.0), axis=1, keepdims=True)
        c_col = jnp.where(row1 < count, c_col, 0.0)
        c_row = jnp.where(lane1 < count, rowform, 0.0)
        e_col = c_col - jnp.sum(gram * c_row, axis=1, keepdims=True)
        e_row = c_row - jnp.sum(gram * c_col, axis=0, keepdims=True)
        t_col, t_row = c_col + e_col, c_row + e_row
        gt_row = jnp.sum(gram * t_col, axis=0, keepdims=True)
        length_sq = self_norm + jnp.sum(t_row * (gt_row - 2.0 * c_row), axis=1, keepdims=True)
        length_sq = jnp.maximum(length_sq, 0.0)
        length = jnp.sqrt(length_sq)
        inverse = 1.0 / jnp.maximum(length, 0.5)
        hcols.append(jnp.where(row1 == count, length, t_col))
        weights = jnp.broadcast_to(t_col * inverse, (ROWS, LANES))
        newest = [tile * inverse for tile in applied]
        for i in range(count):
            weight = jnp.broadcast_to(weights[i:i + 1, :], (by, bz))
            for x in range(bx):
                newest[x] = newest[x] - weight * out[i, x]
        for x in range(bx):
            out[count, x] = newest[x]
        if k == EXPAND - 1:
            break
        halo_wait(halos[k + 1])
        sides = []
        for side in (0, 1):
            near_row, near_lane = (by - 1, bz - 1) if side == 0 else (0, 0)
            factor = scale * inverse if k == 0 else inverse
            x_part = xs[k + 1, side] * factor
            y_part = [ys[k + 1, side, x, near_row:near_row + 1, :] * factor for x in range(bx)]
            y_part = jnp.concatenate(y_part, axis=0)
            for i in range(count):
                weight = weights[i:i + 1, :]
                if i < KEEP:
                    x_part = x_part - weight * xr[side, i]
                    y_part = y_part - weight * yr[side, i]
                else:
                    x_part = x_part - weight * xh[side, i - KEEP]
                    y_part = y_part - weight * yh[side, i - KEEP]
            z_part = []
            for x in range(bx):
                column = (zs[k + 1, side, x, :, near_lane:near_lane + 1] * factor
                          - jnp.sum(zh[side, x] * (t_row * inverse), axis=1, keepdims=True))
                z_part.append(column)
                if k + 1 < EXPAND - 1:
                    zh[side, x] = jnp.where(lane3 == count, column, zh[side, x])
            xh[side, count - KEEP] = x_part
            yh[side, count - KEEP] = y_part
            sides.append((x_part, [y_part[x:x + 1] for x in range(bx)], z_part))
        applied = stencil(newest, sides[0][0], sides[1][0], sides[0][1], sides[1][1],
                          sides[0][2], sides[1][2])
        if k + 1 < EXPAND - 1:
            for x in range(bx):
                image[1, x] = applied[x]
            halos[k + 2] = field_copies(k + 2, image.at[1])
            halo_start(halos[k + 2])
        cross_col = (e_col - jnp.sum(gram * e_row, axis=1, keepdims=True)) * inverse
        cross_row = (e_row - jnp.sum(gram * e_col, axis=0, keepdims=True)) * inverse
        corner = length_sq * inverse * inverse
        gram = jnp.where(row == count, cross_row, jnp.where(lane == count, cross_col, gram))
        gram = jnp.where((row == count) & (lane == count), corner, gram)

    hess[...] = jnp.concatenate(hcols, axis=1)
    halo_finish(halo_w)
    halo_finish(halo_r)
    for copies in halos.values():
        halo_finish(copies)
    for copies in pending:
        for copy in copies:
            copy.wait_send()


def per_device(krylov_basis, schur_vectors, next_vector, diag_shift, velocity):
    sizes = tuple(lax.axis_size(a) for a in AXES)
    block = next_vector.shape
    bx, by, bz = block
    cells = float(bx * by * bz * sizes[0] * sizes[1] * sizes[2])
    n0, n1 = sizes[1] * sizes[2], sizes[0]
    small = EXPAND - 1
    f32 = jnp.float32
    vmem = pl.BlockSpec(memory_space=pltpu.VMEM)
    dma = pltpu.SemaphoreType.DMA
    return pl.pallas_call(
        functools.partial(body, sizes, cells),
        out_shape=(
            jax.ShapeDtypeStruct((ROWS,) + block, f32),
            jax.ShapeDtypeStruct((ROWS, EXPAND), f32),
        ),
        in_specs=[
            pl.BlockSpec(memory_space=pl.ANY),
            pl.BlockSpec(memory_space=pltpu.SMEM),
            vmem, vmem, vmem,
        ],
        out_specs=(vmem, vmem),
        scratch_shapes=[
            pltpu.VMEM(krylov_basis.shape, f32),
            pltpu.VMEM((2,) + block, f32),
            pltpu.VMEM((2, KEEP, by, bz), f32),
            pltpu.VMEM((2, KEEP, bx, bz), f32),
            pltpu.VMEM((2,) + block, f32),
            pltpu.VMEM((2, KEEP, bx, bz), f32),
            pltpu.VMEM((2,) + block, f32),
            pltpu.VMEM((2, EXPAND, by, bz), f32),
            pltpu.VMEM((2, EXPAND, bx, bz), f32),
            pltpu.VMEM((2,) + block, f32),
            pltpu.VMEM((EXPAND, 2, by, bz), f32),
            pltpu.VMEM((EXPAND, 2) + block, f32),
            pltpu.VMEM((EXPAND, 2) + block, f32),
            pltpu.VMEM((2, 8, LANES), f32),
            pltpu.VMEM((n0 - 1, 8, LANES), f32),
            pltpu.VMEM((n1 - 1, 8, LANES), f32),
            pltpu.VMEM((small, 2, 1, LANES), f32),
            pltpu.VMEM((small, n0 - 1, 1, LANES), f32),
            pltpu.VMEM((small, n1 - 1, 1, LANES), f32),
            dma, dma((24,)), dma((24,)),
            dma((n0 - 1,)), dma((n0 - 1,)), dma((n1 - 1,)), dma((n1 - 1,)),
            dma((small, n0 - 1)), dma((small, n0 - 1)),
            dma((small, n1 - 1)), dma((small, n1 - 1)),
        ],
        compiler_params=pltpu.CompilerParams(collective_id=0, has_side_effects=True),
    )(krylov_basis, schur_vectors, next_vector, diag_shift, velocity)


def solution(mesh):
    in_specs = (
        P(None, "gx", "gy", "gz"),
        P(),
        P("gx", "gy", "gz"),
        P("gx", "gy", "gz"),
        P(None, "gx", "gy", "gz"),
    )
    out_specs = (P(None, "gx", "gy", "gz"), P())
    return jax.shard_map(
        per_device, mesh=mesh, in_specs=in_specs, out_specs=out_specs, check_vma=False
    )
```

time: 260 us -> 38.1 us (0.15)
  blocking collectives: 166 us -> 0 us
  starting transfers between devices: 47.2 us -> 0 us
  Pallas kernels: 0 us -> 32.6 us
  waiting for transfers between devices: 19.5 us -> 0 us
  matrix products: 10.7 us -> 0 us
  between operations: 7.79 us -> 0.64 us
  other arithmetic: 3.24 us -> 0 us
    psum x4 -> x0, blocking collectives: 166 us -> none  [the longest x3 124 us: per_device(): lax.psum((jnp.dot(flat_basis, applied, precision=highest), jnp.sum(applie...]
    ppermute x18 -> x0, starting transfers between devices: 47.2 us -> none  [the longest x9 35.6 us: with_halo(): before = lax.ppermute(last, axis, up)]
    pallas_call x0 -> x1, Pallas kernels: none -> 32.6 us  [per_device(): pl.pallas_call(functools.partial(body, sizes, cells), out_shape=(jax.Shap...]
    ppermute x18 -> x0, waiting for transfers between devices: 19.5 us -> none  [the longest x9 13.4 us: with_halo(): after = lax.ppermute(initial, axis, down)]
    dot_general x19 -> x0, matrix products: 10.7 us -> none  [the longest x3 2.25 us: per_device(): jnp.dot(gram_matrix, total_coeffs, precision=highest)]
  transfers between devices with their start and end apart: 18 -> 0, of which waited for: 12 -> 0; matrix products, arithmetic and copies ran while one was open for 0% -> 0% of each run, Pallas kernels for 0% -> 0%
where the time goes in v1:
time: 38.1 us; the launch traced here: 37.7 us
  Pallas kernels  32.6 us (86%)
  local copies, waits for them, and re-layouts  4.54 us (12%)
  between operations  0.64 us (2%)
    pallas_call x1, Pallas kernels, per_device(): pl.pallas_call(functools.partial(body, sizes, cells), out_shape=(jax.Shap...  32.6 us
    unnamed x2, local copies, waits for them, and re-layouts  3.18 us
    pallas_call x1, local copies, waits for them, and re-layouts, per_device(): pl.pallas_call(functools.partial(body, sizes, cells), out_shape=(jax.Shap...  1.36 us

profile of v1, /device:TPU:0, one launch (start us, length us, event | category | flops | bytes accessed | tf_op | source)
XLA Modules:
  0.0 37.7 jit_solution(11954454416148846229)
XLA Ops:
  0.6 1.4 %copy.7.schur = f32[60,20]{1,0:T(8,128)} copy(f32[60,20]{0,1:T(8,128)} %param.6) | data formatting | bytes 9600 | tf_op args[1]
  2.0 32.6 %shard_map.68 = (f32[24,4,8,128]{3,2,1,0:T(8,128)}, f32[24,3]{1,0:T(8,128)}) custom-call(f32[60,4,8,128]{3,2,1,0:T(8,128)} %kry_hbm.1, f32[60,20]{1,0:T(8,128)} %copy.7.schur, f32[4,8,128]{2,1,0:T(8,128)} %w_ref.1, f32[4,8,128]{2,1,0:T(8,128)} %diag.1, f32[3,4,8,128]{3,2,1,0:T(8,128)} %vel.1), custom_call_target="tpu_custom_call" | custom-call | tf_op jit(solution)/shard_map/pallas_call | solution.py:347
  34.6 1.4 %copy.8 = f32[24,3]{0,1:T(4,128)} copy(f32[24,3]{1,0:T(8,128)} %get-tuple-element.3) | data formatting | bytes 576 | tf_op jit(solution)/shard_map/pallas_call | solution.py:347
  36.0 1.8 %copy.10 = f32[24,4,8,128]{3,2,1,0:T(8,128)} copy(f32[24,4,8,128]{3,2,1,0:T(8,128)} %get-tuple-element.6) | data formatting | bytes 786432

commit v2 on v1

--- a/solution.py
+++ b/solution.py
@@ -12,6 +12,7 @@
 ROWS = 24
 LANES = 128
 GROUP = 32
+DIRECT = 64
 AXES = ("gx", "gy", "gz")
 
 
@@ -20,6 +21,9 @@
     nx, ny, nz = sizes
     if phase == 1:
         return (lax.rem(ix + offset, nx), iy, iz)
+    if phase == 2:
+        other = lax.rem((ix * ny + iy) * nz + iz + offset, nx * ny * nz)
+        return (other // (ny * nz), lax.rem(other // nz, ny), lax.rem(other, nz))
     other = lax.rem(iy * nz + iz + offset, ny * nz)
     return (ix, other // nz, lax.rem(other, nz))
 
@@ -29,16 +33,17 @@
     kry_hbm, schur, w_ref, diag, vel,
     out, hess,
     kry, image, xr, yr, zr, ypack, zpack, xh, yh, zh, xs, ys, zs,
-    gsend, grecv0, grecv1, rsend, rrecv0, rrecv1,
+    gsend, grecv0, grecv1, rsend, rrecv0, rrecv1, mid,
     load_sem, halo_send, halo_recv, gsem_s0, gsem_r0, gsem_s1, gsem_r1,
-    rsem_s0, rsem_r0, rsem_s1, rsem_r1,
+    rsem_s0, rsem_r0, rsem_s1, rsem_r1, ready,
 ):
     place = tuple(lax.axis_index(a) for a in AXES)
     basis = kry.shape[0]
     bx, by, bz = w_ref.shape
     load = pltpu.make_async_copy(kry_hbm, kry, load_sem)
     load.start()
-    groups = (sizes[1] * sizes[2], sizes[0])
+    groups = (sizes[1] * sizes[2], sizes[0], sizes[0] * sizes[1] * sizes[2])
+    direct = groups[2] <= DIRECT
 
     for ref in (xr, yr, zr, xs, ys, zs):
         ref[...] = jnp.zeros_like(ref)
@@ -107,9 +112,28 @@
     def gather_sum(copies, own, slots):
         for copy in copies:
             copy.wait_recv()
-        for k in range(len(copies)):
-            own = own + slots[k]
-        return own
+        terms = [own] + [slots[k] for k in range(len(copies))]
+        while len(terms) > 1:
+            terms = [sum(terms[k:k + 2]) for k in range(0, len(terms), 2)]
+        return terms[0]
+
+    pending = []
+
+    def row_start(k, rowform):
+        rsend[k] = rowform
+        phase = 2 if direct else 0
+        copies = exchange(rsend.at[k], rrecv0.at[k], rsem_s0.at[k], rsem_r0.at[k], phase)
+        pending.append(copies)
+        return copies
+
+    def row_end(k, rowform, copies):
+        rowform = gather_sum(copies, rowform, rrecv0.at[k])
+        if not direct:
+            mid[k] = rowform
+            copies = exchange(mid.at[k], rrecv1.at[k], rsem_s1.at[k], rsem_r1.at[k], 1)
+            pending.append(copies)
+            rowform = gather_sum(copies, rowform, rrecv1.at[k])
+        return rowform * (1.0 / cells)
 
     lane3 = lax.broadcasted_iota(jnp.int32, (by, bz), 1)
     row3 = lax.broadcasted_iota(jnp.int32, (by, bz), 0)
@@ -148,6 +172,11 @@
 
     halo_w = field_copies(0, w_ref)
     halo_start(halo_w)
+    if direct:
+        for offset in range(1, groups[1]):
+            pl.semaphore_signal(
+                ready, inc=1, device_id=group_partner(1, offset, place, sizes),
+                device_id_type=pl.DeviceIdType.MESH)
 
     load.wait()
     wide, deep = 5, 4
@@ -159,7 +188,7 @@
                 for x in range(bx):
                     tile = kry[i, x]
                     for j in range(wide):
-                        sums[j * bx + x] = sums[j * bx + x] + schur[i, first + j] * tile
+                        sums[j * bx + x] = sums[j * bx + x] + schur[first + j, i] * tile
             return tuple(sums)
         sums = lax.fori_loop(
             0, basis // deep, step,
@@ -195,6 +224,13 @@
         col = dots([out[j, x] for x in range(bx)], KEEP + 1)
         gram = jnp.where(lane == j, jnp.where(row < KEEP + 1, col, 0.0), gram)
 
+    packed = jnp.zeros((8, LANES), jnp.float32)
+    for part in range(ROWS // 8):
+        piece = gram[part * 8:part * 8 + 8]
+        packed = packed + (pltpu.roll(piece, part * GROUP, 1) if part else piece)
+    gsend[0] = packed
+    gcopies0 = exchange(gsend.at[0], grecv0, gsem_s0, gsem_r0, 0)
+
     halo_wait(halo_w)
     applied = stencil(
         [w_ref[x] for x in range(bx)], xs[0, 0], xs[0, 1],
@@ -205,36 +241,33 @@
     )
     for x in range(bx):
         image[0, x] = applied[x]
+    ownrow = jnp.sum(jnp.where(row == lane, dots(applied, KEEP + 1), 0.0),
+                     axis=0, keepdims=True)
+    if direct:
+        pl.semaphore_wait(ready, groups[1] - 1)
+    copies = row_start(0, ownrow)
     halo_a = field_copies(1, image.at[0])
     halo_start(halo_a)
-    col = dots(applied, KEEP + 1)
-    gram = jnp.where(lane == ROWS - 1, col, gram)
-    packed = jnp.zeros((8, LANES), jnp.float32)
-    for part in range(ROWS // 8):
-        piece = gram[part * 8:part * 8 + 8]
-        packed = packed + (pltpu.roll(piece, part * GROUP, 1) if part else piece)
-    gsend[0] = packed
-    copies0 = exchange(gsend.at[0], grecv0, gsem_s0, gsem_r0, 0)
-    packed = gather_sum(copies0, packed, grecv0)
+
+    packed = gather_sum(gcopies0, packed, grecv0)
     gsend[1] = packed
-    copies1 = exchange(gsend.at[1], grecv1, gsem_s1, gsem_r1, 1)
-    packed = gather_sum(copies1, packed, grecv1) * (1.0 / cells)
-    pending = [copies0, copies1]
+    gcopies1 = exchange(gsend.at[1], grecv1, gsem_s1, gsem_r1, 1)
+    packed = gather_sum(gcopies1, packed, grecv1) * (1.0 / cells)
+    pending += [gcopies0, gcopies1]
     gram = jnp.concatenate(
         [packed] + [pltpu.roll(packed, LANES - part * GROUP, 1) for part in range(1, ROWS // 8)],
         axis=0)
-
-    c_col = jnp.sum(jnp.where(lane == ROWS - 1, gram, 0.0), axis=1, keepdims=True)
     gram = jnp.where((lane < KEEP + 1) & (row < KEEP + 1), gram, 0.0)
     norm_sq = jnp.sum(
         jnp.sum(jnp.where((lane == KEEP) & (row == KEEP), gram, 0.0), axis=1, keepdims=True),
         axis=0, keepdims=True)
     scale = 1.0 / jnp.maximum(jnp.sqrt(norm_sq), 0.5)
     gram = gram * jnp.where(row == KEEP, scale, 1.0) * jnp.where(lane == KEEP, scale, 1.0)
-    c_col = c_col * scale * jnp.where((row1 == KEEP) | (row1 == ROWS - 1), scale, 1.0)
     for x in range(bx):
         out[KEEP, x] = w_ref[x] * scale
     applied = [tile * scale for tile in applied]
+    rowform = row_end(0, ownrow, copies)
+    rowform = rowform * scale * jnp.where((lane1 == KEEP) | (lane1 == ROWS - 1), scale, 1.0)
 
     halo_wait(halo_r)
     for side in (0, 1):
@@ -251,18 +284,8 @@
         if k > 0:
             rowform = jnp.sum(jnp.where(row == lane, dots(applied, count), 0.0),
                               axis=0, keepdims=True)
-            rsend[k - 1, 0] = rowform
-            copies0 = exchange(rsend.at[k - 1, 0], rrecv0.at[k - 1],
-                               rsem_s0.at[k - 1], rsem_r0.at[k - 1], 0)
-            rowform = gather_sum(copies0, rowform, rrecv0.at[k - 1])
-            rsend[k - 1, 1] = rowform
-            copies1 = exchange(rsend.at[k - 1, 1], rrecv1.at[k - 1],
-                               rsem_s1.at[k - 1], rsem_r1.at[k - 1], 1)
-            rowform = gather_sum(copies1, rowform, rrecv1.at[k - 1]) * (1.0 / cells)
-            pending += [copies0, copies1]
-            c_col = jnp.sum(jnp.where(row == lane, rowform, 0.0), axis=1, keepdims=True)
-        else:
-            rowform = jnp.sum(jnp.where(row == lane, c_col, 0.0), axis=0, keepdims=True)
+            rowform = row_end(k, rowform, row_start(k, rowform))
+        c_col = jnp.sum(jnp.where(row == lane, rowform, 0.0), axis=1, keepdims=True)
         self_norm = jnp.sum(jnp.where(lane1 == ROWS - 1, rowform, 0.0), axis=1, keepdims=True)
         c_col = jnp.where(row1 < count, c_col, 0.0)
         c_row = jnp.where(lane1 < count, rowform, 0.0)
@@ -324,7 +347,9 @@
         gram = jnp.where(row == count, cross_row, jnp.where(lane == count, cross_col, gram))
         gram = jnp.where((row == count) & (lane == count), corner, gram)
 
-    hess[...] = jnp.concatenate(hcols, axis=1)
+    for k in range(EXPAND):
+        hess[k:k + 1] = jnp.sum(
+            jnp.where(row == lane, hcols[k % len(hcols)], 0.0), axis=0, keepdims=True)
     halo_finish(halo_w)
     halo_finish(halo_r)
     for copies in halos.values():
@@ -340,15 +365,15 @@
     bx, by, bz = block
     cells = float(bx * by * bz * sizes[0] * sizes[1] * sizes[2])
     n0, n1 = sizes[1] * sizes[2], sizes[0]
-    small = EXPAND - 1
+    nrow = n0 * n1 if n0 * n1 <= DIRECT else n0
     f32 = jnp.float32
     vmem = pl.BlockSpec(memory_space=pltpu.VMEM)
     dma = pltpu.SemaphoreType.DMA
-    return pl.pallas_call(
+    vectors, columns = pl.pallas_call(
         functools.partial(body, sizes, cells),
         out_shape=(
-            jax.ShapeDtypeStruct((ROWS,) + block, f32),
-            jax.ShapeDtypeStruct((ROWS, EXPAND), f32),
+            pltpu.VMEM((ROWS,) + block, f32),
+            pltpu.VMEM((8, LANES), f32),
         ),
         in_specs=[
             pl.BlockSpec(memory_space=pl.ANY),
@@ -373,16 +398,19 @@
             pltpu.VMEM((2, 8, LANES), f32),
             pltpu.VMEM((n0 - 1, 8, LANES), f32),
             pltpu.VMEM((n1 - 1, 8, LANES), f32),
-            pltpu.VMEM((small, 2, 1, LANES), f32),
-            pltpu.VMEM((small, n0 - 1, 1, LANES), f32),
-            pltpu.VMEM((small, n1 - 1, 1, LANES), f32),
+            pltpu.VMEM((EXPAND, 1, LANES), f32),
+            pltpu.VMEM((EXPAND, nrow - 1, 1, LANES), f32),
+            pltpu.VMEM((EXPAND, n1 - 1, 1, LANES), f32),
+            pltpu.VMEM((EXPAND, 1, LANES), f32),
             dma, dma((24,)), dma((24,)),
             dma((n0 - 1,)), dma((n0 - 1,)), dma((n1 - 1,)), dma((n1 - 1,)),
-            dma((small, n0 - 1)), dma((small, n0 - 1)),
-            dma((small, n1 - 1)), dma((small, n1 - 1)),
+            dma((EXPAND, nrow - 1)), dma((EXPAND, nrow - 1)),
+            dma((EXPAND, n1 - 1)), dma((EXPAND, n1 - 1)),
+            pltpu.SemaphoreType.REGULAR,
         ],
         compiler_params=pltpu.CompilerParams(collective_id=0, has_side_effects=True),
-    )(krylov_basis, schur_vectors, next_vector, diag_shift, velocity)
+    )(krylov_basis, schur_vectors.T, next_vector, diag_shift, velocity)
+    return vectors, columns[0:EXPAND, 0:ROWS].T
 
 
 def solution(mesh):

time: 38.1 us -> 31 us (0.81)
  Pallas kernels: 32.6 us -> 28.9 us
  local copies, waits for them, and re-layouts: 4.54 us -> 1.33 us
    pallas_call x1, Pallas kernels: 32.6 us -> 28.9 us  [per_device(): pl.pallas_call(functools.partial(body, sizes, cells), out_shape=(pltpu.VM...]
    unnamed x2 -> x1, local copies, waits for them, and re-layouts: 3.18 us -> 0.75 us
    pallas_call x1 -> x0, local copies, waits for them, and re-layouts: 1.36 us -> none  [per_device(): pl.pallas_call(functools.partial(body, sizes, cells), out_shape=(jax.Shap...]
    transpose x0 -> x1, local copies, waits for them, and re-layouts: none -> 0.58 us  [per_device(): return (vectors, columns[0:EXPAND, 0:ROWS].T)]
where the time goes in v2:
time: 31 us; the launch traced here: 30.9 us
  Pallas kernels  28.9 us (93%)
  local copies, waits for them, and re-layouts  1.33 us (4%)
  between operations  0.64 us (2%)
    pallas_call x1, Pallas kernels, per_device(): pl.pallas_call(functools.partial(body, sizes, cells), out_shape=(pltpu.VM...  28.9 us
    unnamed x1, local copies, waits for them, and re-layouts  0.75 us

profile of v2, /device:TPU:0, one launch (start us, length us, event | category | flops | bytes accessed | tf_op | source)
XLA Modules:
  0.0 30.9 jit_solution(5342886649683424215)
XLA Ops:
  0.6 28.9 %shard_map.68 = (f32[24,4,8,128]{3,2,1,0:T(8,128)S(1)}, f32[8,128]{1,0:T(8,128)S(1)}) custom-call(f32[60,4,8,128]{3,2,1,0:T(8,128)} %kry_hbm.1, f32[20,60]{1,0:T(8,128)} %bitcast.3, f32[4,8,128]{2,1,0:T(8,128)} %w_ref.1, f32[4,8,128]{2,1,0:T(8,128)} %diag.1, f32[3,4,8,128]{3,2,1,0:T(8,128)} %vel.1), custom_call_target="tpu_custom_call" | custom-call | tf_op jit(solution)/shard_map/pallas_call | solution.py:372
  29.5 0.7 %copy.8 = f32[24,4,8,128]{3,2,1,0:T(8,128)} copy(f32[24,4,8,128]{3,2,1,0:T(8,128)S(1)} %get-tuple-element.6) | data formatting | bytes 786432
  30.3 0.6 %slice_bitcast_fusion = f32[24,3]{0,1:T(4,128)} fusion(f32[8,128]{1,0:T(8,128)S(1)} %get-tuple-element.5), kind=kLoop, calls=%fused_computation | loop fusion | bytes 576 | tf_op jit(solution)/shard_map/transpose | solution.py:413

commit v3 on v2

--- a/solution.py
+++ b/solution.py
@@ -16,23 +16,19 @@
 AXES = ("gx", "gy", "gz")
 
 
-def group_partner(phase, offset, place, sizes):
-    ix, iy, iz = place
-    nx, ny, nz = sizes
-    if phase == 1:
-        return (lax.rem(ix + offset, nx), iy, iz)
-    if phase == 2:
-        other = lax.rem((ix * ny + iy) * nz + iz + offset, nx * ny * nz)
-        return (other // (ny * nz), lax.rem(other // nz, ny), lax.rem(other, nz))
-    other = lax.rem(iy * nz + iz + offset, ny * nz)
-    return (ix, other // nz, lax.rem(other, nz))
+def partner_steps(phase, sizes):
+    xs = range(1, sizes[0]) if phase else ()
+    steps = [(dx, 0, 0) for dx in xs] if phase == 1 else [
+        (dx, dy, dz) for dx in tuple(xs) + (0,)
+        for dy in range(sizes[1]) for dz in range(sizes[2])]
+    return [step for step in steps if step != (0, 0, 0)]
 
 
 def body(
     sizes, cells,
-    kry_hbm, schur, w_ref, diag, vel,
+    kry_hbm, schur_hbm, w_hbm, diag_hbm, vel_hbm,
     out, hess,
-    kry, image, xr, yr, zr, ypack, zpack, xh, yh, zh, xs, ys, zs,
+    schur, w_ref, diag, vel, kry, image, xr, yr, zr, ypack, zpack, xh, yh, zh, xs, ys, zs,
     gsend, grecv0, grecv1, rsend, rrecv0, rrecv1, mid,
     load_sem, halo_send, halo_recv, gsem_s0, gsem_r0, gsem_s1, gsem_r1,
     rsem_s0, rsem_r0, rsem_s1, rsem_r1, ready,
@@ -40,25 +36,29 @@
     place = tuple(lax.axis_index(a) for a in AXES)
     basis = kry.shape[0]
     bx, by, bz = w_ref.shape
-    load = pltpu.make_async_copy(kry_hbm, kry, load_sem)
-    load.start()
-    groups = (sizes[1] * sizes[2], sizes[0], sizes[0] * sizes[1] * sizes[2])
-    direct = groups[2] <= DIRECT
+    loads = [
+        pltpu.make_async_copy(source, target, load_sem.at[k])
+        for k, (source, target) in enumerate((
+            (w_hbm, w_ref), (schur_hbm, schur), (kry_hbm, kry), (diag_hbm, diag), (vel_hbm, vel)))
+    ]
+    for copy in loads:
+        copy.start()
+    direct = sizes[0] * sizes[1] * sizes[2] <= DIRECT
+    shifted = [[lax.rem(place[d] + k, sizes[d]) for k in range(sizes[d])] for d in range(3)]
+
+    def partners(phase):
+        return [tuple(shifted[d][step[d]] for d in range(3))
+                for step in partner_steps(phase, sizes)]
+
 
     for ref in (xr, yr, zr, xs, ys, zs):
         ref[...] = jnp.zeros_like(ref)
-    out[KEEP + 1:ROWS] = jnp.zeros((ROWS - KEEP - 1, bx, by, bz), jnp.float32)
-    out[KEEP] = w_ref[...]
 
     barrier = pltpu.get_barrier_semaphore()
-    for phase in (0, 1):
-        for offset in range(1, groups[phase]):
-            pl.semaphore_signal(
-                barrier, inc=1,
-                device_id=group_partner(phase, offset, place, sizes),
-                device_id_type=pl.DeviceIdType.MESH,
-            )
-    pl.semaphore_wait(barrier, groups[0] + groups[1] - 2)
+    for to in partners(0) + partners(1):
+        pl.semaphore_signal(
+            barrier, inc=1, device_id=to, device_id_type=pl.DeviceIdType.MESH)
+    pl.semaphore_wait(barrier, len(partners(0)) + len(partners(1)))
 
     def halo_copies(kind, sources, targets):
         found = []
@@ -98,12 +98,11 @@
 
     def exchange(send, slots, sems_s, sems_r, phase):
         copies = []
-        for offset in range(1, groups[phase]):
+        for at, to in enumerate(partners(phase)):
             copies.append(pltpu.make_async_remote_copy(
-                src_ref=send, dst_ref=slots.at[offset - 1],
-                send_sem=sems_s.at[offset - 1], recv_sem=sems_r.at[offset - 1],
-                device_id=group_partner(phase, offset, place, sizes),
-                device_id_type=pl.DeviceIdType.MESH,
+                src_ref=send, dst_ref=slots.at[at],
+                send_sem=sems_s.at[at], recv_sem=sems_r.at[at],
+                device_id=to, device_id_type=pl.DeviceIdType.MESH,
             ))
         for copy in copies:
             copy.start()
@@ -171,14 +170,17 @@
         return jnp.sum(jnp.concatenate(parts, axis=0), axis=1, keepdims=True)
 
     halo_w = field_copies(0, w_ref)
+    loads[0].wait()
     halo_start(halo_w)
     if direct:
-        for offset in range(1, groups[1]):
+        for to in partners(1):
             pl.semaphore_signal(
-                ready, inc=1, device_id=group_partner(1, offset, place, sizes),
-                device_id_type=pl.DeviceIdType.MESH)
-
-    load.wait()
+                ready, inc=1, device_id=to, device_id_type=pl.DeviceIdType.MESH)
+
+    out[KEEP + 1:ROWS] = jnp.zeros((ROWS - KEEP - 1, bx, by, bz), jnp.float32)
+    out[KEEP] = w_ref[...]
+    loads[1].wait()
+    loads[2].wait()
     wide, deep = 5, 4
     for first in range(0, KEEP, wide):
         def step(at, sums, first=first):
@@ -231,6 +233,8 @@
     gsend[0] = packed
     gcopies0 = exchange(gsend.at[0], grecv0, gsem_s0, gsem_r0, 0)
 
+    loads[3].wait()
+    loads[4].wait()
     halo_wait(halo_w)
     applied = stencil(
         [w_ref[x] for x in range(bx)], xs[0, 0], xs[0, 1],
@@ -244,7 +248,7 @@
     ownrow = jnp.sum(jnp.where(row == lane, dots(applied, KEEP + 1), 0.0),
                      axis=0, keepdims=True)
     if direct:
-        pl.semaphore_wait(ready, groups[1] - 1)
+        pl.semaphore_wait(ready, sizes[0] - 1)
     copies = row_start(0, ownrow)
     halo_a = field_copies(1, image.at[0])
     halo_start(halo_a)
@@ -285,25 +289,25 @@
             rowform = jnp.sum(jnp.where(row == lane, dots(applied, count), 0.0),
                               axis=0, keepdims=True)
             rowform = row_end(k, rowform, row_start(k, rowform))
-        c_col = jnp.sum(jnp.where(row == lane, rowform, 0.0), axis=1, keepdims=True)
-        self_norm = jnp.sum(jnp.where(lane1 == ROWS - 1, rowform, 0.0), axis=1, keepdims=True)
-        c_col = jnp.where(row1 < count, c_col, 0.0)
         c_row = jnp.where(lane1 < count, rowform, 0.0)
-        e_col = c_col - jnp.sum(gram * c_row, axis=1, keepdims=True)
-        e_row = c_row - jnp.sum(gram * c_col, axis=0, keepdims=True)
-        t_col, t_row = c_col + e_col, c_row + e_row
-        gt_row = jnp.sum(gram * t_col, axis=0, keepdims=True)
-        length_sq = self_norm + jnp.sum(t_row * (gt_row - 2.0 * c_row), axis=1, keepdims=True)
+        twice = jnp.where(row == lane, 2.0, 0.0) - gram
+        t_col = jnp.sum(twice * c_row, axis=1, keepdims=True)
+        weights = jnp.broadcast_to(t_col, (ROWS, LANES))
+        t_row = jnp.sum(jnp.where(row == lane, weights, 0.0), axis=0, keepdims=True)
+        gt_row = jnp.sum(gram * weights, axis=0, keepdims=True)
+        length_sq = jnp.sum(
+            jnp.where(lane1 == ROWS - 1, rowform, t_row * (gt_row - 2.0 * c_row)),
+            axis=1, keepdims=True)
         length_sq = jnp.maximum(length_sq, 0.0)
         length = jnp.sqrt(length_sq)
         inverse = 1.0 / jnp.maximum(length, 0.5)
-        hcols.append(jnp.where(row1 == count, length, t_col))
-        weights = jnp.broadcast_to(t_col * inverse, (ROWS, LANES))
-        newest = [tile * inverse for tile in applied]
+        hcols.append(jnp.where(lane1 == count, length, t_row))
+        newest = list(applied)
         for i in range(count):
             weight = jnp.broadcast_to(weights[i:i + 1, :], (by, bz))
             for x in range(bx):
                 newest[x] = newest[x] - weight * out[i, x]
+        newest = [tile * inverse for tile in newest]
         for x in range(bx):
             out[count, x] = newest[x]
         if k == EXPAND - 1:
@@ -312,7 +316,7 @@
         sides = []
         for side in (0, 1):
             near_row, near_lane = (by - 1, bz - 1) if side == 0 else (0, 0)
-            factor = scale * inverse if k == 0 else inverse
+            factor = scale if k == 0 else 1.0
             x_part = xs[k + 1, side] * factor
             y_part = [ys[k + 1, side, x, near_row:near_row + 1, :] * factor for x in range(bx)]
             y_part = jnp.concatenate(y_part, axis=0)
@@ -324,10 +328,12 @@
                 else:
                     x_part = x_part - weight * xh[side, i - KEEP]
                     y_part = y_part - weight * yh[side, i - KEEP]
+            x_part = x_part * inverse
+            y_part = y_part * inverse
             z_part = []
             for x in range(bx):
                 column = (zs[k + 1, side, x, :, near_lane:near_lane + 1] * factor
-                          - jnp.sum(zh[side, x] * (t_row * inverse), axis=1, keepdims=True))
+                          - jnp.sum(zh[side, x] * t_row, axis=1, keepdims=True)) * inverse
                 z_part.append(column)
                 if k + 1 < EXPAND - 1:
                     zh[side, x] = jnp.where(lane3 == count, column, zh[side, x])
@@ -341,6 +347,8 @@
                 image[1, x] = applied[x]
             halos[k + 2] = field_copies(k + 2, image.at[1])
             halo_start(halos[k + 2])
+        e_row = t_row - c_row
+        e_col = jnp.sum(jnp.where(row == lane, e_row, 0.0), axis=1, keepdims=True)
         cross_col = (e_col - jnp.sum(gram * e_row, axis=1, keepdims=True)) * inverse
         cross_row = (e_row - jnp.sum(gram * e_col, axis=0, keepdims=True)) * inverse
         corner = length_sq * inverse * inverse
@@ -348,8 +356,7 @@
         gram = jnp.where((row == count) & (lane == count), corner, gram)
 
     for k in range(EXPAND):
-        hess[k:k + 1] = jnp.sum(
-            jnp.where(row == lane, hcols[k % len(hcols)], 0.0), axis=0, keepdims=True)
+        hess[k:k + 1] = hcols[k % len(hcols)]
     halo_finish(halo_w)
     halo_finish(halo_r)
     for copies in halos.values():
@@ -376,12 +383,14 @@
             pltpu.VMEM((8, LANES), f32),
         ),
         in_specs=[
-            pl.BlockSpec(memory_space=pl.ANY),
-            pl.BlockSpec(memory_space=pltpu.SMEM),
-            vmem, vmem, vmem,
+            pl.BlockSpec(memory_space=pl.ANY) for _ in range(5)
         ],
         out_specs=(vmem, vmem),
         scratch_shapes=[
+            pltpu.SMEM(schur_vectors.shape[::-1], f32),
+            pltpu.VMEM(block, f32),
+            pltpu.VMEM(block, f32),
+            pltpu.VMEM((3,) + block, f32),
             pltpu.VMEM(krylov_basis.shape, f32),
             pltpu.VMEM((2,) + block, f32),
             pltpu.VMEM((2, KEEP, by, bz), f32),
@@ -402,7 +411,7 @@
             pltpu.VMEM((EXPAND, nrow - 1, 1, LANES), f32),
             pltpu.VMEM((EXPAND, n1 - 1, 1, LANES), f32),
             pltpu.VMEM((EXPAND, 1, LANES), f32),
-            dma, dma((24,)), dma((24,)),
+            dma((5,)), dma((24,)), dma((24,)),
             dma((n0 - 1,)), dma((n0 - 1,)), dma((n1 - 1,)), dma((n1 - 1,)),
             dma((EXPAND, nrow - 1)), dma((EXPAND, nrow - 1)),
             dma((EXPAND, n1 - 1)), dma((EXPAND, n1 - 1)),

time: 31 us -> 30.1 us (0.971)
  Pallas kernels: 28.9 us -> 28 us
    pallas_call x1, Pallas kernels: 28.9 us -> 28 us  [per_device(): pl.pallas_call(functools.partial(body, sizes, cells), out_shape=(pltpu.VM...]
where the time goes in v3:
time: 30.1 us; the launch traced here: 29.9 us
  Pallas kernels  28 us (93%)
  local copies, waits for them, and re-layouts  1.33 us (4%)
  between operations  0.64 us (2%)
    pallas_call x1, Pallas kernels, per_device(): pl.pallas_call(functools.partial(body, sizes, cells), out_shape=(pltpu.VM...  28 us
    unnamed x1, local copies, waits for them, and re-layouts  0.75 us

profile of v3, /device:TPU:0, one launch (start us, length us, event | category | flops | bytes accessed | tf_op | source)
XLA Modules:
  0.0 29.9 jit_solution(14009963650288751682)
XLA Ops:
  0.6 28.0 %shard_map.68 = (f32[24,4,8,128]{3,2,1,0:T(8,128)S(1)}, f32[8,128]{1,0:T(8,128)S(1)}) custom-call(f32[60,4,8,128]{3,2,1,0:T(8,128)} %kry_hbm.1, f32[20,60]{1,0:T(8,128)} %bitcast.3, f32[4,8,128]{2,1,0:T(8,128)} %w_hbm.1, f32[4,8,128]{2,1,0:T(8,128)} %diag_hbm.1, f32[3,4,8,128]{3,2,1,0:T(8,128)} %vel_hbm.1), custom_call_target="tpu_custom_call" | custom-call | tf_op jit(solution)/shard_map/pallas_call | solution.py:379
  28.6 0.7 %copy.8 = f32[24,4,8,128]{3,2,1,0:T(8,128)} copy(f32[24,4,8,128]{3,2,1,0:T(8,128)S(1)} %get-tuple-element.6) | data formatting | bytes 786432
  29.4 0.6 %slice_bitcast_fusion = f32[24,3]{0,1:T(4,128)} fusion(f32[8,128]{1,0:T(8,128)S(1)} %get-tuple-element.5), kind=kLoop, calls=%fused_computation | loop fusion | bytes 576 | tf_op jit(solution)/shard_map/transpose | solution.py:422

commit v4 on v3

--- a/solution.py
+++ b/solution.py
@@ -19,7 +19,7 @@
 def partner_steps(phase, sizes):
     xs = range(1, sizes[0]) if phase else ()
     steps = [(dx, 0, 0) for dx in xs] if phase == 1 else [
-        (dx, dy, dz) for dx in tuple(xs) + (0,)
+        (dx, dy, dz) for dx in tuple(reversed(xs)) + (0,)
         for dy in range(sizes[1]) for dz in range(sizes[2])]
     return [step for step in steps if step != (0, 0, 0)]
 
@@ -96,42 +96,39 @@
             tuple((r.at[kind, 0], r.at[kind, 1]) for r in (xs, ys, zs)),
         )
 
-    def exchange(send, slots, sems_s, sems_r, phase):
-        copies = []
+    def exchange(send, slots, sem_s, sem_r, phase):
         for at, to in enumerate(partners(phase)):
-            copies.append(pltpu.make_async_remote_copy(
-                src_ref=send, dst_ref=slots.at[at],
-                send_sem=sems_s.at[at], recv_sem=sems_r.at[at],
+            pltpu.make_async_remote_copy(
+                src_ref=send, dst_ref=slots.at[at], send_sem=sem_s, recv_sem=sem_r,
                 device_id=to, device_id_type=pl.DeviceIdType.MESH,
-            ))
-        for copy in copies:
-            copy.start()
-        return copies
-
-    def gather_sum(copies, own, slots):
-        for copy in copies:
-            copy.wait_recv()
-        terms = [own] + [slots[k] for k in range(len(copies))]
+            ).start()
+        pending.append(pltpu.make_async_copy(slots, slots, sem_s))
+        return pltpu.make_async_copy(slots, slots, sem_r)
+
+    def gather_sum(arrival, own, slots):
+        arrival.wait()
+        terms = [own] + [slots[k] for k in range(slots.shape[0])]
         while len(terms) > 1:
-            terms = [sum(terms[k:k + 2]) for k in range(0, len(terms), 2)]
+            terms = [sum(terms[k + 1:k + 2], terms[k]) for k in range(0, len(terms), 2)]
         return terms[0]
 
     pending = []
+
+    def finish_sends():
+        while pending:
+            pending.pop().wait()
 
     def row_start(k, rowform):
         rsend[k] = rowform
-        phase = 2 if direct else 0
-        copies = exchange(rsend.at[k], rrecv0.at[k], rsem_s0.at[k], rsem_r0.at[k], phase)
-        pending.append(copies)
-        return copies
-
-    def row_end(k, rowform, copies):
-        rowform = gather_sum(copies, rowform, rrecv0.at[k])
+        return exchange(rsend.at[k], rrecv0.at[k], rsem_s0.at[k], rsem_r0.at[k],
+                        2 if direct else 0)
+
+    def row_end(k, rowform, arrival):
+        rowform = gather_sum(arrival, rowform, rrecv0.at[k])
         if not direct:
             mid[k] = rowform
-            copies = exchange(mid.at[k], rrecv1.at[k], rsem_s1.at[k], rsem_r1.at[k], 1)
-            pending.append(copies)
-            rowform = gather_sum(copies, rowform, rrecv1.at[k])
+            arrival = exchange(mid.at[k], rrecv1.at[k], rsem_s1.at[k], rsem_r1.at[k], 1)
+            rowform = gather_sum(arrival, rowform, rrecv1.at[k])
         return rowform * (1.0 / cells)
 
     lane3 = lax.broadcasted_iota(jnp.int32, (by, bz), 1)
@@ -231,7 +228,7 @@
         piece = gram[part * 8:part * 8 + 8]
         packed = packed + (pltpu.roll(piece, part * GROUP, 1) if part else piece)
     gsend[0] = packed
-    gcopies0 = exchange(gsend.at[0], grecv0, gsem_s0, gsem_r0, 0)
+    arrival0 = exchange(gsend.at[0], grecv1, gsem_s1, gsem_r1, 1)
 
     loads[3].wait()
     loads[4].wait()
@@ -253,11 +250,10 @@
     halo_a = field_copies(1, image.at[0])
     halo_start(halo_a)
 
-    packed = gather_sum(gcopies0, packed, grecv0)
+    packed = gather_sum(arrival0, packed, grecv1)
     gsend[1] = packed
-    gcopies1 = exchange(gsend.at[1], grecv1, gsem_s1, gsem_r1, 1)
-    packed = gather_sum(gcopies1, packed, grecv1) * (1.0 / cells)
-    pending += [gcopies0, gcopies1]
+    arrival1 = exchange(gsend.at[1], grecv0, gsem_s0, gsem_r0, 0)
+    packed = gather_sum(arrival1, packed, grecv0) * (1.0 / cells)
     gram = jnp.concatenate(
         [packed] + [pltpu.roll(packed, LANES - part * GROUP, 1) for part in range(1, ROWS // 8)],
         axis=0)
@@ -282,13 +278,22 @@
             zh[side, x] = jnp.where(
                 lane3 == KEEP, zs[0, side, x, :, near_lane:near_lane + 1] * scale, zr[side, x])
     halos = {1: halo_a}
+    done = [halo_w, halo_r, halo_a]
     hcols = []
     for k in range(EXPAND):
         count = KEEP + 1 + k
         if k > 0:
             rowform = jnp.sum(jnp.where(row == lane, dots(applied, count), 0.0),
                               axis=0, keepdims=True)
-            rowform = row_end(k, rowform, row_start(k, rowform))
+            earlier = pending[:]
+            pending.clear()
+            arrival = row_start(k, rowform)
+            for copy in earlier:
+                copy.wait()
+            for copies in done:
+                halo_finish(copies)
+            done = []
+            rowform = row_end(k, rowform, arrival)
         c_row = jnp.where(lane1 < count, rowform, 0.0)
         twice = jnp.where(row == lane, 2.0, 0.0) - gram
         t_col = jnp.sum(twice * c_row, axis=1, keepdims=True)
@@ -347,6 +352,7 @@
                 image[1, x] = applied[x]
             halos[k + 2] = field_copies(k + 2, image.at[1])
             halo_start(halos[k + 2])
+            done.append(halos[k + 2])
         e_row = t_row - c_row
         e_col = jnp.sum(jnp.where(row == lane, e_row, 0.0), axis=1, keepdims=True)
         cross_col = (e_col - jnp.sum(gram * e_row, axis=1, keepdims=True)) * inverse
@@ -357,13 +363,9 @@
 
     for k in range(EXPAND):
         hess[k:k + 1] = hcols[k % len(hcols)]
-    halo_finish(halo_w)
-    halo_finish(halo_r)
-    for copies in halos.values():
+    for copies in done:
         halo_finish(copies)
-    for copies in pending:
-        for copy in copies:
-            copy.wait_send()
+    finish_sends()
 
 
 def per_device(krylov_basis, schur_vectors, next_vector, diag_shift, velocity):
@@ -412,9 +414,8 @@
             pltpu.VMEM((EXPAND, n1 - 1, 1, LANES), f32),
             pltpu.VMEM((EXPAND, 1, LANES), f32),
             dma((5,)), dma((24,)), dma((24,)),
-            dma((n0 - 1,)), dma((n0 - 1,)), dma((n1 - 1,)), dma((n1 - 1,)),
-            dma((EXPAND, nrow - 1)), dma((EXPAND, nrow - 1)),
-            dma((EXPAND, n1 - 1)), dma((EXPAND, n1 - 1)),
+            dma, dma, dma, dma,
+            dma((EXPAND,)), dma((EXPAND,)), dma((EXPAND,)), dma((EXPAND,)),
             pltpu.SemaphoreType.REGULAR,
         ],
         compiler_params=pltpu.CompilerParams(collective_id=0, has_side_effects=True),

time: 30.1 us -> 28.6 us (0.950)
  Pallas kernels: 28 us -> 26.4 us
    pallas_call x1, Pallas kernels: 28 us -> 26.4 us  [per_device(): pl.pallas_call(functools.partial(body, sizes, cells), out_shape=(pltpu.VM...]
where the time goes in v4:
time: 28.6 us; the launch traced here: 28.4 us
  Pallas kernels  26.4 us (92%)
  local copies, waits for them, and re-layouts  1.33 us (5%)
  between operations  0.64 us (2%)
    pallas_call x1, Pallas kernels, per_device(): pl.pallas_call(functools.partial(body, sizes, cells), out_shape=(pltpu.VM...  26.4 us
    unnamed x1, local copies, waits for them, and re-layouts  0.75 us
    transpose x1, local copies, waits for them, and re-layouts, per_device(): return (vectors, columns[0:EXPAND, 0:ROWS].T)  0.58 us

profile of v4, /device:TPU:0, one launch (start us, length us, event | category | flops | bytes accessed | tf_op | source)
XLA Modules:
  0.0 28.4 jit_solution(13981266406423841079)
XLA Ops:
  0.6 26.4 %shard_map.68 = (f32[24,4,8,128]{3,2,1,0:T(8,128)S(1)}, f32[8,128]{1,0:T(8,128)S(1)}) custom-call(f32[60,4,8,128]{3,2,1,0:T(8,128)} %kry_hbm.1, f32[20,60]{1,0:T(8,128)} %bitcast.3, f32[4,8,128]{2,1,0:T(8,128)} %w_hbm.1, f32[4,8,128]{2,1,0:T(8,128)} %diag_hbm.1, f32[3,4,8,128]{3,2,1,0:T(8,128)} %vel_hbm.1), custom_call_target="tpu_custom_call" | custom-call | tf_op jit(solution)/shard_map/pallas_call | solution.py:381
  27.1 0.7 %copy.8 = f32[24,4,8,128]{3,2,1,0:T(8,128)} copy(f32[24,4,8,128]{3,2,1,0:T(8,128)S(1)} %get-tuple-element.6) | data formatting | bytes 786432
  27.8 0.6 %slice_bitcast_fusion = f32[24,3]{0,1:T(4,128)} fusion(f32[8,128]{1,0:T(8,128)S(1)} %get-tuple-element.5), kind=kLoop, calls=%fused_computation | loop fusion | bytes 576 | tf_op jit(solution)/shard_map/transpose | solution.py:423

commit v5 on v4

--- a/solution.py
+++ b/solution.py
@@ -11,7 +11,7 @@
 EXPAND = 3
 ROWS = 24
 LANES = 128
-GROUP = 32
+UNIT = 16
 DIRECT = 64
 AXES = ("gx", "gy", "gz")
 
@@ -149,10 +149,10 @@
             res.append((6.0 + diag[x]) * here - neighbours + 0.5 * flow)
         return res
 
-    def dots(v, count):
+    def dots(v, count, first=0):
         parts = []
         for i in range(ROWS):
-            if i < count:
+            if first <= i < count:
                 total = out[i, 0] * v[0]
                 for x in range(1, bx):
                     total = total + out[i, x] * v[x]
@@ -211,7 +211,6 @@
          (zpack.at[0], zpack.at[1])),
         tuple((r.at[0], r.at[1]) for r in (xr, yr, zr)),
     )
-    halo_start(halo_r)
 
     row = lax.broadcasted_iota(jnp.int32, (ROWS, LANES), 0)
     lane = lax.broadcasted_iota(jnp.int32, (ROWS, LANES), 1)
@@ -220,15 +219,29 @@
 
     gram = jnp.zeros((ROWS, LANES), jnp.float32)
     for j in range(KEEP + 1):
-        col = dots([out[j, x] for x in range(bx)], KEEP + 1)
-        gram = jnp.where(lane == j, jnp.where(row < KEEP + 1, col, 0.0), gram)
-
-    packed = jnp.zeros((8, LANES), jnp.float32)
-    for part in range(ROWS // 8):
-        piece = gram[part * 8:part * 8 + 8]
-        packed = packed + (pltpu.roll(piece, part * GROUP, 1) if part else piece)
+        col = dots([out[j, x] for x in range(bx)], KEEP + 1, j // 8 * 8)
+        gram = jnp.where((lane == j) & (row < KEEP + 1), col, gram)
+    lane8 = lax.broadcasted_iota(jnp.int32, (8, LANES), 1)
+    own8 = lane8 // UNIT == lax.broadcasted_iota(jnp.int32, (8, LANES), 0)
+
+    def spread(value):
+        for shift in (UNIT, 2 * UNIT, 4 * UNIT):
+            value = value + pltpu.roll(value, shift, 1)
+        return value
+
+    units = (
+        gram[16:24],
+        gram[8:16],
+        jnp.where(lane8 < 8, gram[0:8], pltpu.roll(gram[16:24], LANES - 8, 1)),
+    )
+    packed = jnp.concatenate([
+        jnp.sum(jnp.where(own8, spread(jnp.where(lane8 < UNIT, unit, 0.0)), 0.0),
+                axis=0, keepdims=True)
+        for unit in units], axis=0)
     gsend[0] = packed
-    arrival0 = exchange(gsend.at[0], grecv1, gsem_s1, gsem_r1, 1)
+    if direct:
+        pl.semaphore_wait(ready, sizes[0] - 1)
+    arrival0 = exchange(gsend.at[0], grecv1, gsem_s1, gsem_r1, 2 if direct else 1)
 
     loads[3].wait()
     loads[4].wait()
@@ -244,19 +257,29 @@
         image[0, x] = applied[x]
     ownrow = jnp.sum(jnp.where(row == lane, dots(applied, KEEP + 1), 0.0),
                      axis=0, keepdims=True)
-    if direct:
-        pl.semaphore_wait(ready, sizes[0] - 1)
     copies = row_start(0, ownrow)
     halo_a = field_copies(1, image.at[0])
     halo_start(halo_a)
+    halo_start(halo_r)
 
     packed = gather_sum(arrival0, packed, grecv1)
-    gsend[1] = packed
-    arrival1 = exchange(gsend.at[1], grecv0, gsem_s0, gsem_r0, 0)
-    packed = gather_sum(arrival1, packed, grecv0) * (1.0 / cells)
+    if not direct:
+        gsend[1] = packed
+        arrival1 = exchange(gsend.at[1], grecv0, gsem_s0, gsem_r0, 0)
+        packed = gather_sum(arrival1, packed, grecv0)
+    packed = packed * (1.0 / cells)
+    units = [
+        jnp.where(lane8 < UNIT,
+                  spread(jnp.where(own8, jnp.broadcast_to(packed[u:u + 1], (8, LANES)), 0.0)),
+                  0.0)
+        for u in range(3)]
+    corner = pltpu.roll(jnp.where(lane8 >= 8, units[2], 0.0), 8, 1)
+    below = jnp.concatenate(
+        [jnp.zeros((8, LANES), jnp.float32), jnp.where(lane8 < 8, units[1], 0.0), units[0],
+         jnp.zeros((LANES - ROWS, LANES), jnp.float32)], axis=0)
     gram = jnp.concatenate(
-        [packed] + [pltpu.roll(packed, LANES - part * GROUP, 1) for part in range(1, ROWS // 8)],
-        axis=0)
+        [jnp.where(lane8 < 8, units[2], 0.0), units[1], units[0] + corner], axis=0)
+    gram = gram + below.T[0:ROWS]
     gram = jnp.where((lane < KEEP + 1) & (row < KEEP + 1), gram, 0.0)
     norm_sq = jnp.sum(
         jnp.sum(jnp.where((lane == KEEP) & (row == KEEP), gram, 0.0), axis=1, keepdims=True),
@@ -375,6 +398,7 @@
     cells = float(bx * by * bz * sizes[0] * sizes[1] * sizes[2])
     n0, n1 = sizes[1] * sizes[2], sizes[0]
     nrow = n0 * n1 if n0 * n1 <= DIRECT else n0
+    nline = n0 * n1 if n0 * n1 <= DIRECT else n1
     f32 = jnp.float32
     vmem = pl.BlockSpec(memory_space=pltpu.VMEM)
     dma = pltpu.SemaphoreType.DMA
@@ -406,9 +430,9 @@
             pltpu.VMEM((EXPAND, 2, by, bz), f32),
             pltpu.VMEM((EXPAND, 2) + block, f32),
             pltpu.VMEM((EXPAND, 2) + block, f32),
-            pltpu.VMEM((2, 8, LANES), f32),
-            pltpu.VMEM((n0 - 1, 8, LANES), f32),
-            pltpu.VMEM((n1 - 1, 8, LANES), f32),
+            pltpu.VMEM((2, 3, LANES), f32),
+            pltpu.VMEM((n0 - 1, 3, LANES), f32),
+            pltpu.VMEM((nline - 1, 3, LANES), f32),
             pltpu.VMEM((EXPAND, 1, LANES), f32),
             pltpu.VMEM((EXPAND, nrow - 1, 1, LANES), f32),
             pltpu.VMEM((EXPAND, n1 - 1, 1, LANES), f32),

time: 28.6 us -> 26.7 us (0.934)
  Pallas kernels: 26.4 us -> 24.6 us
    pallas_call x1, Pallas kernels: 26.4 us -> 24.6 us  [per_device(): pl.pallas_call(functools.partial(body, sizes, cells), out_shape=(pltpu.VM...]
where the time goes in v5:
time: 26.7 us; the launch traced here: 26.5 us
  Pallas kernels  24.6 us (92%)
  local copies, waits for them, and re-layouts  1.33 us (5%)
  between operations  0.64 us (2%)
    pallas_call x1, Pallas kernels, per_device(): pl.pallas_call(functools.partial(body, sizes, cells), out_shape=(pltpu.VM...  24.6 us
    unnamed x1, local copies, waits for them, and re-layouts  0.75 us
    transpose x1, local copies, waits for them, and re-layouts, per_device(): return (vectors, columns[0:EXPAND, 0:ROWS].T)  0.58 us

profile of v5, /device:TPU:0, one launch (start us, length us, event | category | flops | bytes accessed | tf_op | source)
XLA Modules:
  0.0 26.5 jit_solution(13718520891674820305)
XLA Ops:
  0.6 24.6 %shard_map.68 = (f32[24,4,8,128]{3,2,1,0:T(8,128)S(1)}, f32[8,128]{1,0:T(8,128)S(1)}) custom-call(f32[60,4,8,128]{3,2,1,0:T(8,128)} %kry_hbm.1, f32[20,60]{1,0:T(8,128)} %bitcast.3, f32[4,8,128]{2,1,0:T(8,128)} %w_hbm.1, f32[4,8,128]{2,1,0:T(8,128)} %diag_hbm.1, f32[3,4,8,128]{3,2,1,0:T(8,128)} %vel_hbm.1), custom_call_target="tpu_custom_call" | custom-call | tf_op jit(solution)/shard_map/pallas_call | solution.py:405
  25.2 0.7 %copy.8 = f32[24,4,8,128]{3,2,1,0:T(8,128)} copy(f32[24,4,8,128]{3,2,1,0:T(8,128)S(1)} %get-tuple-element.6) | data formatting | bytes 786432
  26.0 0.6 %slice_bitcast_fusion = f32[24,3]{0,1:T(4,128)} fusion(f32[8,128]{1,0:T(8,128)S(1)} %get-tuple-element.5), kind=kLoop, calls=%fused_computation | loop fusion | bytes 576 | tf_op jit(solution)/shard_map/transpose | solution.py:447

commit v6 on v5

--- a/solution.py
+++ b/solution.py
@@ -196,22 +196,6 @@
             for x in range(bx):
                 out[first + j, x] = sums[j * bx + x]
 
-    for side, (row, edge) in enumerate(((by - 1, bz - 1), (0, 0))):
-        for i in range(KEEP):
-            ypack[side, i] = out[i, :, row, :]
-        for x in range(bx):
-            packed = jnp.zeros((by, bz), jnp.float32)
-            for i in range(KEEP):
-                packed = jnp.where(
-                    lane3 == i, pltpu.roll(out[i, x], (i - edge) % bz, 1), packed)
-            zpack[side, x] = packed
-    halo_r = halo_copies(
-        3,
-        ((out.at[0:KEEP, bx - 1], out.at[0:KEEP, 0]), (ypack.at[0], ypack.at[1]),
-         (zpack.at[0], zpack.at[1])),
-        tuple((r.at[0], r.at[1]) for r in (xr, yr, zr)),
-    )
-
     row = lax.broadcasted_iota(jnp.int32, (ROWS, LANES), 0)
     lane = lax.broadcasted_iota(jnp.int32, (ROWS, LANES), 1)
     lane1 = lax.broadcasted_iota(jnp.int32, (1, LANES), 1)
@@ -260,6 +244,22 @@
     copies = row_start(0, ownrow)
     halo_a = field_copies(1, image.at[0])
     halo_start(halo_a)
+
+    for side, (near, edge) in enumerate(((by - 1, bz - 1), (0, 0))):
+        for i in range(KEEP):
+            ypack[side, i] = out[i, :, near, :]
+        for x in range(bx):
+            face = jnp.zeros((by, bz), jnp.float32)
+            for i in range(KEEP):
+                face = jnp.where(
+                    lane3 == i, pltpu.roll(out[i, x], (i - edge) % bz, 1), face)
+            zpack[side, x] = face
+    halo_r = halo_copies(
+        3,
+        ((out.at[0:KEEP, bx - 1], out.at[0:KEEP, 0]), (ypack.at[0], ypack.at[1]),
+         (zpack.at[0], zpack.at[1])),
+        tuple((r.at[0], r.at[1]) for r in (xr, yr, zr)),
+    )
     halo_start(halo_r)
 
     packed = gather_sum(arrival0, packed, grecv1)

time: 26.7 us -> 26.5 us (level)
  no operation moved by 1% of the time
where the time goes in v6:
time: 26.5 us; the launch traced here: 26.4 us
  Pallas kernels  24.4 us (92%)
  local copies, waits for them, and re-layouts  1.33 us (5%)
  between operations  0.64 us (2%)
    pallas_call x1, Pallas kernels, per_device(): pl.pallas_call(functools.partial(body, sizes, cells), out_shape=(pltpu.VM...  24.4 us
    unnamed x1, local copies, waits for them, and re-layouts  0.75 us
    transpose x1, local copies, waits for them, and re-layouts, per_device(): return (vectors, columns[0:EXPAND, 0:ROWS].T)  0.58 us

profile of v6, /device:TPU:0, one launch (start us, length us, event | category | flops | bytes accessed | tf_op | source)
XLA Modules:
  0.0 26.4 jit_solution(16378273145687143570)
XLA Ops:
  0.6 24.4 %shard_map.68 = (f32[24,4,8,128]{3,2,1,0:T(8,128)S(1)}, f32[8,128]{1,0:T(8,128)S(1)}) custom-call(f32[60,4,8,128]{3,2,1,0:T(8,128)} %kry_hbm.1, f32[20,60]{1,0:T(8,128)} %bitcast.3, f32[4,8,128]{2,1,0:T(8,128)} %w_hbm.1, f32[4,8,128]{2,1,0:T(8,128)} %diag_hbm.1, f32[3,4,8,128]{3,2,1,0:T(8,128)} %vel_hbm.1), custom_call_target="tpu_custom_call" | custom-call | tf_op jit(solution)/shard_map/pallas_call | solution.py:405
  25.0 0.7 %copy.8 = f32[24,4,8,128]{3,2,1,0:T(8,128)} copy(f32[24,4,8,128]{3,2,1,0:T(8,128)S(1)} %get-tuple-element.6) | data formatting | bytes 786432
  25.8 0.6 %slice_bitcast_fusion = f32[24,3]{0,1:T(4,128)} fusion(f32[8,128]{1,0:T(8,128)S(1)} %get-tuple-element.5), kind=kLoop, calls=%fused_computation | loop fusion | bytes 576 | tf_op jit(solution)/shard_map/transpose | solution.py:447
